TPU v7x, 32 devices: a whole 2x2x4 slice. The times are simulated.
32 devices in a mesh: dp: 8 (over y, x, core), proto: 4 (over z).
Axes of the slice: x: 2, y: 2, z: 4, core: 2. Of those that a mesh axis runs over, the one named last changes fastest.
Arguments:
- hidden_states: bfloat16 [64, 256, 2048], P(('dp', 'proto')), may hold values from -15 to 30, as said below
- teacher_feats: bfloat16 [64, 256, 384], P(('dp', 'proto')), may hold values from -25 to 25, as said below
- masks: int32 [64, 32], P(('dp', 'proto')), may hold values from 0 to 255, as said below
- head_weight: bfloat16 [2048, 384], replicated, as said below
- prototypes: bfloat16 [49152, 384], P('proto'), may hold values from -25 to 25, as said below
- center: float32 [49152], P('proto'), may hold values from -1.8 to 1.8
Outputs:
- loss: float32 [], replicated
- grad_hidden: bfloat16 [2048, 2048], P(('dp', 'proto'))
- grad_head: float32 [2048, 384], P(('dp', 'proto'))
Inputs may be any that keep to these rules, and one draw needn't show every extreme that they name: `masks`: each row lists 32 different patch numbers of its image. `hidden_states`: independent entries. `teacher_feats`: independent entries. `head_weight`: independent entries of deviation 2048 ** -0.5. `prototypes`: independent entries.
All inputs are finite; a program needn't handle non-finite values.
Results may differ from a plain program's by a relative error of at most 0.00305.
The roundings to bfloat16 on the way count: a program that leaves them out, or rounds other values in their place, can miss the bound.
Values may be sent and summed in bfloat16 or wider, within the bound.
No kernel may reach another device: no remote copies, remote signals or barrier semaphores. Data moves between devices by JAX's collectives and lax.ppermute only.
A program may use at most 64 MiB of HBM per device.

v0:
```python
import math

import jax
import jax.numpy as jnp
from jax import lax
from jax.sharding import PartitionSpec as P

STUDENT_TEMP = 0.1
TEACHER_TEMP = 0.07
LOSS_SCALE = 524288.0
EPSILON = 1e-06


def unit_rows(feats):
    radius = jnp.sqrt(jnp.sum(feats * feats, axis=-1, keepdims=True) + EPSILON)
    return (feats / radius, radius)


def block_logits(student, teacher, protos, center, first, width):
    tile = lax.dynamic_slice_in_dim(protos, first, width, 0)
    offset = lax.dynamic_slice_in_dim(center, first, width, 0)
    dims = (((1,), (1,)), ((), ()))
    s_logits = (
        lax.dot_general(student, tile, dims, preferred_element_type=jnp.float32) / STUDENT_TEMP
    )
    t_logits = (
        lax.dot_general(teacher, tile, dims, preferred_element_type=jnp.float32) - offset[None, :]
    ) / TEACHER_TEMP
    return (s_logits, t_logits, tile)


def row_stats(student, teacher, protos, center):
    count = student.shape[0]
    width = math.gcd(protos.shape[0], 1536)

    def row_step(index, state):
        peak_s, total_s, peak_t, total_t, cross = state
        s_logits, t_logits, tile = block_logits(
            student, teacher, protos, center, index * width, width
        )
        new_s = jnp.maximum(peak_s, jnp.max(s_logits, axis=1))
        total_s = total_s * jnp.exp(peak_s - new_s) + jnp.sum(
            jnp.exp(s_logits - new_s[:, None]), axis=1
        )
        new_t = jnp.maximum(peak_t, jnp.max(t_logits, axis=1))
        weights = jnp.exp(t_logits - new_t[:, None])
        rescale = jnp.exp(peak_t - new_t)
        total_t = total_t * rescale + jnp.sum(weights, axis=1)
        cross = cross * rescale + jnp.sum(weights * s_logits, axis=1)
        return (new_s, total_s, new_t, total_t, cross)

    lowest = jnp.full((count,), -jnp.inf, jnp.float32)
    zeros = jnp.zeros((count,), jnp.float32)
    return lax.fori_loop(
        0, protos.shape[0] // width, row_step, (lowest, zeros, lowest, zeros, zeros)
    )


def per_device(hidden_states, teacher_feats, masks, head_weight, prototypes, center):
    local_rows = masks.shape[0] * masks.shape[1]
    picked = jnp.take_along_axis(hidden_states, masks[:, :, None], axis=1).reshape(
        local_rows, hidden_states.shape[2]
    )
    teacher_rows = jnp.take_along_axis(teacher_feats, masks[:, :, None], axis=1).reshape(
        local_rows, teacher_feats.shape[2]
    )
    raw = jnp.dot(picked, head_weight, preferred_element_type=jnp.float32)
    unit, radius = unit_rows(raw)
    student = unit.astype(jnp.bfloat16)
    teacher = unit_rows(teacher_rows.astype(jnp.float32))[0].astype(jnp.bfloat16)
    bottleneck = head_weight.shape[1]
    group = lax.axis_size("proto")
    group_rows = local_rows * group
    total_rows = group_rows * lax.axis_size("dp")
    factor = LOSS_SCALE / (total_rows * STUDENT_TEMP)
    width = math.gcd(prototypes.shape[0], 1536)
    blocks = prototypes.shape[0] // width
    piece = (
        lax.all_gather(student, "proto", axis=0, tiled=True),
        lax.all_gather(teacher, "proto", axis=0, tiled=True),
    )
    found = row_stats(piece[0], piece[1], prototypes, center)
    collect_stu_all = piece[0]
    collect_tea_all = piece[1]
    collect_peak_s = found[0]
    collect_total_s = found[1]
    collect_peak_t = found[2]
    collect_total_t = found[3]
    cross = found[4]
    stu_all, tea_all, peak_s, total_s, peak_t, total_t, cross = (
        collect_stu_all,
        collect_tea_all,
        collect_peak_s,
        collect_total_s,
        collect_peak_t,
        collect_total_t,
        cross,
    )
    high_s, high_t = lax.pmax((peak_s, peak_t), "proto")
    rescale_t = jnp.exp(peak_t - high_t)
    total_s, total_t, cross = lax.psum(
        (total_s * jnp.exp(peak_s - high_s), total_t * rescale_t, cross * rescale_t), "proto"
    )
    peak_s, peak_t = (high_s, high_t)
    row_loss = peak_s + jnp.log(total_s) - cross / total_t
    loss = lax.psum(jnp.sum(row_loss), "dp") / total_rows
    top_s = peak_s[:, None]
    sum_s = total_s[:, None]
    top_t = peak_t[:, None]
    sum_t = total_t[:, None]

    def gradient_step(index, acc):
        s_logits, t_logits, tile = block_logits(
            stu_all, tea_all, prototypes, center, index * width, width
        )
        prob = jnp.exp(s_logits - top_s) / sum_s
        target = jnp.exp(t_logits - top_t) / sum_t
        grads = (factor * (prob - target)).astype(jnp.bfloat16)
        return acc + jnp.dot(grads, tile, preferred_element_type=jnp.float32)

    back = lax.psum_scatter(
        lax.fori_loop(
            0,
            blocks,
            gradient_step,
            jnp.zeros((local_rows * lax.axis_size("proto"), bottleneck), jnp.float32),
        ),
        "proto",
        scatter_dimension=0,
        tiled=True,
    )
    inner = jnp.sum(unit * back, axis=-1, keepdims=True)
    direction = ((back - unit * inner) / radius).astype(jnp.bfloat16)
    grad_hidden = lax.dot_general(
        direction, head_weight, (((1,), (1,)), ((), ())), preferred_element_type=jnp.float32
    ).astype(jnp.bfloat16)
    grad_head = lax.psum_scatter(
        lax.dot_general(
            picked, direction, (((0,), (0,)), ((), ())), preferred_element_type=jnp.float32
        ),
        ("dp", "proto"),
        scatter_dimension=0,
        tiled=True,
    )
    return (loss, grad_hidden, grad_head)


def solution(mesh):
    return jax.shard_map(
        per_device,
        mesh=mesh,
        in_specs=(
            P(("dp", "proto"), None, None),
            P(("dp", "proto"), None, None),
            P(("dp", "proto"), None),
            P(),
            P("proto", None),
            P("proto"),
        ),
        out_specs=(P(), P(("dp", "proto"), None), P(("dp", "proto"), None)),
        check_vma=False,
    )
```

profile of v0, /device:TPU:0, one launch (start us, length us, event | category | flops | bytes accessed | tf_op | source)
XLA Modules:
  0.0 312.9 jit_solution(12547895231451667666)
XLA Ops:
  7.2 0.8 compare_and_fusion
  8.9 1.5 gather_fusion
  10.4 1.9 multiply_reduce_fusion.3
  12.5 15.5 %all_gather.6 = bf16[256,384]{1,0:T(8,128)(2,1)S(1)} all-gather(bf16[64,384]{1,0:T(8,128)(2,1)S(1)} %fusion.39), channel_id=1, replica_groups=mesh['dp'=8,'proto'=4] {'proto'}, dimensions={0}, use_global_device_ids=true | all-gather | bytes 245760 | tf_op jit(solution)/shard_map/all_gather | solution.py:79
  28.0 1.9 gather_fusion.1
  30.2 14.0 %all_gather.7 = bf16[256,384]{1,0:T(8,128)(2,1)S(1)} all-gather(bf16[64,384]{1,0:T(8,128)(2,1)S(1)} %divide_convert_fusion.1), channel_id=1, replica_groups=mesh['dp'=8,'proto'=4] {'proto'}, dimensions={0}, use_global_device_ids=true | all-gather | bytes 245760 | tf_op jit(solution)/shard_map/all_gather | solution.py:80
  44.2 51.5 %while.36 = (s32[]{:T(128)}, f32[256]{0:T(256)S(1)}, f32[256]{0:T(256)S(1)}, f32[256]{0:T(256)S(1)}, f32[256]{0:T(256)S(1)}, /*index=5*/f32[256]{0:T(256)S(1)}, ...) while((s32[]{:T(128)}, f32[256]{0:T(256)S(1)}, ...), condition=%wide.region_8.9_spmd.clone, body=%wide.region_2.8_spmd.clone.sunk | while | flops 608308224 | bytes 15384807 | solution.py:54
  45.0 3.0 fusion.65
  48.0 2.0 fusion.63
  51.4 3.0 fusion.65
  54.5 2.0 fusion.63
  57.9 3.0 fusion.65
  60.9 2.0 fusion.63
  64.3 3.0 fusion.65
  67.4 2.0 fusion.63
  70.8 3.0 fusion.65
  73.8 2.0 fusion.63
  77.2 3.0 fusion.65
  80.3 2.0 fusion.63
  83.7 3.0 fusion.65
  86.7 2.0 fusion.63
  90.1 3.0 fusion.65
  93.1 2.0 fusion.63
  95.7 11.7 %all-reduce.1 = (f32[256]{0:T(256)S(1)}, f32[256]{0:T(256)S(1)}) all-reduce(f32[256]{0:T(256)S(1)} %get-tuple-element.348, f32[256]{0:T(256)S(1)} %get-tuple-element.345), channel_id=1, replica_groups=mesh['dp'=8,'proto'=4] {'proto'}, use_global_device_ids=true, to_apply=%region_11.12 | all-reduce | flops 512 | bytes 4096 | tf_op jit(solution)/shard_map/pmax | solution.py:99
  107.4 8.4 %all-reduce = (f32[256]{0:T(256)S(1)}, f32[256]{0:T(256)S(1)}, f32[256]{0:T(256)S(1)}) all-reduce(f32[256]{0:T(256)S(1)} %get-tuple-element.473, f32[256]{0:T(256)S(1)} %get-tuple-element.472, f32[256]{0:T(256)S(1)} %get-tuple-element.476), channel_id=1, replica_groups=mesh['dp'=8,'proto'=4] {'proto'}, use_global_device_ids=true, to_apply=%region_12.13 | all-reduce | flops 768 | bytes 6144 | tf_op jit(solution)/shard_map/psum | solution.py:101
  115.8 61.3 %while.37 = (s32[]{:T(128)}, f32[256,384]{1,0:T(8,128)S(1)}, bf16[12288,384]{1,0:T(8,128)(2,1)}, bf16[256,384]{1,0:T(8,128)(2,1)S(1)}, f32[256,1]{0,1:T(1,128)S(...) while((s32[]{:T(128)}, f32[256,384]{1,0:T(8,128)S(1)}, ...), condition=%wide.region_17.18_spmd.clone, body=%wide.region_16.17_spmd.clone.sunk | while | flops 910098432 | bytes 7888580 | solution.py:122
  116.6 3.0 fusion.73
  119.6 3.8 %convolution_add_fusion.2 = f32[256,384]{1,0:T(8,128)S(1)} fusion(f32[1536,256]{1,0:T(8,128)} %fusion.73, bf16[256,384]{1,0:T(8,128)(2,1)S(1)} %get-tuple-element.692, bf16[12288,384]{1,0:T(8,128)(2,1)} %get-tuple-element.691, s32[]{:T(128)S(6)} %select_n.60, f32[256]{0:T(256)S(1)} %bitcast.45, f32[256]{0:T(256)S(1)} %bitcast.37, ...), kind=kOutput, calls=%fused_computation.36.clone.1 | convolution fusion | flops 606535680 | bytes 4918784 | tf_op jit(solution)/shard_map/while/body/eval_jaxpr/dot_general | solution.py:119
  124.3 3.0 fusion.73
  127.3 3.8 %convolution_add_fusion.2 = f32[256,384]{1,0:T(8,128)S(1)} fusion(f32[1536,256]{1,0:T(8,128)} %fusion.73, bf16[256,384]{1,0:T(8,128)(2,1)S(1)} %get-tuple-element.692, bf16[12288,384]{1,0:T(8,128)(2,1)} %get-tuple-element.691, s32[]{:T(128)S(6)} %select_n.60, f32[256]{0:T(256)S(1)} %bitcast.45, f32[256]{0:T(256)S(1)} %bitcast.37, ...), kind=kOutput, calls=%fused_computation.36.clone.1 | convolution fusion | flops 606535680 | bytes 4918784 | tf_op jit(solution)/shard_map/while/body/eval_jaxpr/dot_general | solution.py:119
  131.9 3.0 fusion.73
  134.9 3.9 %convolution_add_fusion.2 = f32[256,384]{1,0:T(8,128)S(1)} fusion(f32[1536,256]{1,0:T(8,128)} %fusion.73, bf16[256,384]{1,0:T(8,128)(2,1)S(1)} %get-tuple-element.692, bf16[12288,384]{1,0:T(8,128)(2,1)} %get-tuple-element.691, s32[]{:T(128)S(6)} %select_n.60, f32[256]{0:T(256)S(1)} %bitcast.45, f32[256]{0:T(256)S(1)} %bitcast.37, ...), kind=kOutput, calls=%fused_computation.36.clone.1 | convolution fusion | flops 606535680 | bytes 4918784 | tf_op jit(solution)/shard_map/while/body/eval_jaxpr/dot_general | solution.py:119
  139.6 3.0 fusion.73
  142.6 3.8 %convolution_add_fusion.2 = f32[256,384]{1,0:T(8,128)S(1)} fusion(f32[1536,256]{1,0:T(8,128)} %fusion.73, bf16[256,384]{1,0:T(8,128)(2,1)S(1)} %get-tuple-element.692, bf16[12288,384]{1,0:T(8,128)(2,1)} %get-tuple-element.691, s32[]{:T(128)S(6)} %select_n.60, f32[256]{0:T(256)S(1)} %bitcast.45, f32[256]{0:T(256)S(1)} %bitcast.37, ...), kind=kOutput, calls=%fused_computation.36.clone.1 | convolution fusion | flops 606535680 | bytes 4918784 | tf_op jit(solution)/shard_map/while/body/eval_jaxpr/dot_general | solution.py:119
  147.3 3.0 fusion.73
  150.3 3.8 %convolution_add_fusion.2 = f32[256,384]{1,0:T(8,128)S(1)} fusion(f32[1536,256]{1,0:T(8,128)} %fusion.73, bf16[256,384]{1,0:T(8,128)(2,1)S(1)} %get-tuple-element.692, bf16[12288,384]{1,0:T(8,128)(2,1)} %get-tuple-element.691, s32[]{:T(128)S(6)} %select_n.60, f32[256]{0:T(256)S(1)} %bitcast.45, f32[256]{0:T(256)S(1)} %bitcast.37, ...), kind=kOutput, calls=%fused_computation.36.clone.1 | convolution fusion | flops 606535680 | bytes 4918784 | tf_op jit(solution)/shard_map/while/body/eval_jaxpr/dot_general | solution.py:119
  154.9 3.0 fusion.73
  158.0 3.8 %convolution_add_fusion.2 = f32[256,384]{1,0:T(8,128)S(1)} fusion(f32[1536,256]{1,0:T(8,128)} %fusion.73, bf16[256,384]{1,0:T(8,128)(2,1)S(1)} %get-tuple-element.692, bf16[12288,384]{1,0:T(8,128)(2,1)} %get-tuple-element.691, s32[]{:T(128)S(6)} %select_n.60, f32[256]{0:T(256)S(1)} %bitcast.45, f32[256]{0:T(256)S(1)} %bitcast.37, ...), kind=kOutput, calls=%fused_computation.36.clone.1 | convolution fusion | flops 606535680 | bytes 4918784 | tf_op jit(solution)/shard_map/while/body/eval_jaxpr/dot_general | solution.py:119
  162.6 3.0 fusion.73
  165.6 3.8 %convolution_add_fusion.2 = f32[256,384]{1,0:T(8,128)S(1)} fusion(f32[1536,256]{1,0:T(8,128)} %fusion.73, bf16[256,384]{1,0:T(8,128)(2,1)S(1)} %get-tuple-element.692, bf16[12288,384]{1,0:T(8,128)(2,1)} %get-tuple-element.691, s32[]{:T(128)S(6)} %select_n.60, f32[256]{0:T(256)S(1)} %bitcast.45, f32[256]{0:T(256)S(1)} %bitcast.37, ...), kind=kOutput, calls=%fused_computation.36.clone.1 | convolution fusion | flops 606535680 | bytes 4918784 | tf_op jit(solution)/shard_map/while/body/eval_jaxpr/dot_general | solution.py:119
  170.2 3.0 fusion.73
  173.3 3.8 %convolution_add_fusion.2 = f32[256,384]{1,0:T(8,128)S(1)} fusion(f32[1536,256]{1,0:T(8,128)} %fusion.73, bf16[256,384]{1,0:T(8,128)(2,1)S(1)} %get-tuple-element.692, bf16[12288,384]{1,0:T(8,128)(2,1)} %get-tuple-element.691, s32[]{:T(128)S(6)} %select_n.60, f32[256]{0:T(256)S(1)} %bitcast.45, f32[256]{0:T(256)S(1)} %bitcast.37, ...), kind=kOutput, calls=%fused_computation.36.clone.1 | convolution fusion | flops 606535680 | bytes 4918784 | tf_op jit(solution)/shard_map/while/body/eval_jaxpr/dot_general | solution.py:119
  177.9 20.6 %reduce-scatter.3.cloned.1.call-done = f32[64,384]{1,0:T(8,128)} async-done(((f32[256,384]{1,0:T(8,128)}), f32[64,384]{1,0:T(8,128)}) %reduce-scatter.3.cloned.1.call-update) | async-done | bytes 98320 | tf_op jit(solution)/shard_map/reduce_scatter | solution.py:121
  198.5 1.1 multiply_reduce_fusion.1
  199.6 3.3 %fusion.33 = f32[2048,384]{1,0:T(8,128)} fusion(bf16[64,2048]{1,0:T(8,128)(2,1)S(1)} %gather_fusion, pred[64]{0:T(512)(128)(4,1)S(1)} %broadcast_in_dim.62, f32[64,384]{1,0:T(8,128)} %reduce-scatter.3.cloned.1.call-done, f32[64]{0:T(128)S(1)} %multiply_reduce_fusion.1, f32[64]{0:T(128)S(1)} %add_sqrt_fusion.1, f32[64,384]{1,0:T(8,128)S(1)} %get-tuple-element.475), kind=kOutput, calls=%fused_computation.49 | convolution fusion | flops 100917248 | bytes 3605056 | tf_op jit(solution)/shard_map/dot_general | solution.py:138
  203.5 12.4 %psum.31 = f32[]{:T(128)} all-reduce(f32[]{:T(128)} %subtract_reduce_fusion), channel_id=1, replica_groups=mesh['dp'=8,'proto'=4] {'dp'}, use_global_device_ids=true, to_apply=%region_15.16 | all-reduce | flops 1 | bytes 8 | tf_op jit(solution)/shard_map/psum | solution.py:106
  216.6 2.8 convolution_convert_fusion
  219.4 85.6 %reduce-scatter.5.cloned.1.call-done = f32[64,384]{1,0:T(8,128)} async-done(((f32[2048,384]{1,0:T(8,128)}), f32[64,384]{1,0:T(8,128)}) %reduce-scatter.5.cloned.1.call-update) | async-done | bytes 98320 | tf_op jit(solution)/shard_map/reduce_scatter | solution.py:137
  (107 shorter events, 20.0 us)
Async XLA Ops:
  7.2 1.8 copy-start
  7.2 191.4 %reduce-scatter.3.cloned.1.call-start = ((), (), s32[]{:S(2)}) async-start(), calls=%async_computation.2 | async-start | bytes 491520 | tf_op jit(solution)/shard_map/reduce_scatter | solution.py:121
  48.0 2.0 copy-start.1
  54.5 2.0 copy-start.1
  60.9 2.0 copy-start.1
  67.4 2.0 copy-start.1
  73.8 2.0 copy-start.1
  80.2 2.0 copy-start.1
  86.7 2.0 copy-start.1
  93.1 2.0 copy-start.1
  177.1 0.7 copy-start.3
  177.9 127.1 %reduce-scatter.5.cloned.1.call-start = ((), (), s32[]{:S(2)}) async-start(), calls=%async_computation.3 | async-start | bytes 3244032 | tf_op jit(solution)/shard_map/reduce_scatter | solution.py:137
  202.9 13.7 %copy-start.2 = (f32[64,384]{1,0:T(8,128)S(1)}, f32[64,384]{1,0:T(8,128)}, u32[]{:S(2)}) copy-start(f32[64,384]{1,0:T(8,128)} %reduce-scatter.3.cloned.1.call-done) | copy-start | bytes 294916
Sparse Core Ops, SparseCore 0:
  178.0 20.5 reduce-scatter.2
  204.5 100.3 reduce-scatter.4
where the time goes:
time: 315 us; the launch traced here: 313 us
  waiting for transfers between devices  106 us (34%)
  matrix products  103 us (33%)
  blocking collectives  62 us (20%)
  local copies, waits for them, and re-layouts  17 us (5%)
  between operations  15.9 us (5%)
  other arithmetic  8.1 us (3%)
    reduce_scatter x1, waiting for transfers between devices, per_device(): lax.psum_scatter(lax.dot_general(picked, direction, (((0,), (0,)), ((), (...  85.6 us
    dot_general x16, matrix products, block_logits(): lax.dot_general(teacher, tile, dims, preferred_element_type=jnp.float32)  48.5 us
    dot_general x8, matrix products, gradient_step(): return acc + jnp.dot(grads, tile, preferred_element_type=jnp.float32)  30.5 us
    reduce_scatter x1, waiting for transfers between devices, per_device(): lax.psum_scatter(lax.fori_loop(0, blocks, gradient_step, jnp.zeros((local...  20.6 us
    dot_general x8, matrix products, block_logits(): lax.dot_general(student, tile, dims, preferred_element_type=jnp.float32)  15.9 us
    all_gather x1, blocking collectives, per_device(): lax.all_gather(student, 'proto', axis=0, tiled=True)  15.5 us
    all_gather x1, blocking collectives, per_device(): lax.all_gather(teacher, 'proto', axis=0, tiled=True)  14 us
    dynamic_slice x16, local copies, waits for them, and re-layouts, block_logits(): offset = lax.dynamic_slice_in_dim(center, first, width, 0)  12.6 us
  transfers between devices with their start and end apart: 2, of which 2 were waited for; matrix products, arithmetic and copies ran while one was open for 1% of the time, Pallas kernels for 0%

commit v1 on v0

v1 whole, which is shorter than its diff:
```python
import functools
import math

import jax
import jax.numpy as jnp
from jax import lax
from jax.experimental import pallas as pl
from jax.experimental.pallas import tpu as pltpu
from jax.sharding import PartitionSpec as P


STUDENT_TEMP = 0.1
TEACHER_TEMP = 0.07
LOSS_SCALE = 524288.0
EPSILON = 1e-06
LOG2E = math.log2(math.e)
LN2 = math.log(2.0)
SCALE_S = LOG2E / STUDENT_TEMP
SCALE_T = LOG2E / TEACHER_TEMP
LANES = 128
NT = (((1,), (1,)), ((), ()))
TN = (((0,), (0,)), ((), ()))
F32 = jnp.float32
BF16 = jnp.bfloat16
VMEM = pl.BlockSpec(memory_space=pltpu.VMEM)
HBM = pl.BlockSpec(memory_space=pltpu.HBM)


def dot(a, b, dims=(((1,), (0,)), ((), ()))):
    return lax.dot_general(a, b, dims, preferred_element_type=F32)


def params(mib):
    return pltpu.CompilerParams(vmem_limit_bytes=mib * 2**20)


def cost(flops, nbytes):
    return pl.CostEstimate(flops=int(flops), bytes_accessed=int(nbytes), transcendentals=0)


def shapes(*specs):
    return tuple(jax.ShapeDtypeStruct(s, d) for s, d in specs)


def pick_kernel(dp, hidden_hbm, feats_hbm, masks_hbm, weight_hbm, rows_out, unit_out, radius_out, *refs):
    cols_out, (hidden, feats, masks, weight, picked_out, sems) = refs[:dp], refs[dp:]
    images, patches, _ = hidden.shape
    fetches = [
        pltpu.make_async_copy(source, target, sems.at[index])
        for index, (source, target) in enumerate(
            [(masks_hbm, masks), (feats_hbm, feats)]
            + [(hidden_hbm.at[image], hidden.at[image]) for image in range(images)]
            + [(weight_hbm, weight)]
        )
    ]
    for fetch in fetches:
        fetch.start()
    fetches[0].wait()
    fetches[1].wait()
    count = masks.shape[1]
    rows = images * count
    patch = lax.broadcasted_iota(jnp.int32, (patches, count), 0)
    for image in range(images):
        here = slice(image * count, (image + 1) * count)
        choice = (patch == masks[image : image + 1, :]).astype(F32).T.astype(BF16)
        fetches[2 + image].wait()
        picked_out[here, :] = dot(choice, hidden[image]).astype(BF16)
        feat = dot(choice, feats[image])
        length = jnp.sqrt(jnp.sum(feat * feat, axis=1, keepdims=True) + EPSILON)
        rows_out[rows + image * count : rows + (image + 1) * count, :] = (feat / length).astype(BF16)
    fetches[2 + images].wait()
    raw = dot(picked_out[...], weight[...])
    radius = jnp.sqrt(jnp.sum(raw * raw, axis=1, keepdims=True) + EPSILON)
    unit = raw / radius
    unit_out[...] = unit
    radius_out[...] = jnp.broadcast_to(radius, radius_out.shape)
    rows_out[0:rows, :] = unit.astype(BF16)
    me = lax.axis_index("dp")
    width = cols_out[0].shape[1]
    for k in range(dp):
        first = pl.multiple_of(jnp.bitwise_xor(me, k) * width, LANES)
        cols_out[k][...] = picked_out[:, pl.ds(first, width)]


def stats_kernel(parts, block, unroll, fetch, *refs):
    inputs = parts + (2 if fetch else 3)
    row_refs, (source, center, *done) = refs[:parts], refs[parts:inputs]
    logits, stats = refs[inputs : inputs + 2]
    protos, scratch = source, refs[inputs + 2 :]
    if fetch:
        protos, sems, *scratch = scratch
    both, tops, sums, cross = scratch
    count = source.shape[0] // block
    ahead = min(3, count)

    def copy(number):
        piece = pl.ds(pl.multiple_of(number * block, block), block)
        return pltpu.make_async_copy(source.at[piece], protos.at[piece], sems.at[number])

    if fetch:
        for number in range(ahead):
            copy(number).start()
    each = row_refs[0].shape[0] // 2
    rows = parts * each
    for index, ref in enumerate(row_refs):
        both[index * each : (index + 1) * each, :] = ref[0:each, :]
        both[rows + index * each : rows + (index + 1) * each, :] = ref[each:, :]
    tops[...] = jnp.full(tops.shape, -jnp.inf, F32)
    sums[...] = jnp.zeros(sums.shape, F32)
    cross[...] = jnp.zeros(cross.shape, F32)
    groups = block // LANES
    chunk = 8

    def project(base, number, u):
        if fetch:
            copy(number + u).wait()
            pl.when(number + u + ahead < count)(lambda: copy(number + u + ahead).start())
        piece = protos[pl.ds(base + u * block, block), :]
        logits[:, pl.ds(base + u * block, block)] = dot(both[...], piece, NT)

    def reduce(base, u):
        lanes = [pl.ds(base + u * block + g * LANES, LANES) for g in range(groups)]
        offset = [center[:, lane] * SCALE_T for lane in lanes]
        for start in range(0, rows, chunk):
            srow = slice(start, start + chunk)
            trow = slice(rows + start, rows + start + chunk)
            s = [logits[srow, lane] * SCALE_S for lane in lanes]
            t = [logits[trow, lane] * SCALE_T - offset[g] for g, lane in enumerate(lanes)]
            old_s, old_t = tops[srow, :], tops[trow, :]
            new_s = functools.reduce(jnp.maximum, s, old_s)
            new_t = functools.reduce(jnp.maximum, t, old_t)
            tops[srow, :] = new_s
            tops[trow, :] = new_t
            fade = jnp.exp2(old_t - new_t)
            e_t = [jnp.exp2(x - new_t) for x in t]
            sums[srow, :] = sums[srow, :] * jnp.exp2(old_s - new_s) + sum(jnp.exp2(x - new_s) for x in s)
            sums[trow, :] = sums[trow, :] * fade + sum(e_t)
            cross[srow, :] = cross[srow, :] * fade + sum(e * x for e, x in zip(e_t, s))

    def step(index, carry):
        base = pl.multiple_of(index * (unroll * block), unroll * block)
        for u in range(unroll):
            project(base, index * unroll, u)
            if u > 0:
                reduce(base, u - 1)
        reduce(base, unroll - 1)
        return carry

    lax.fori_loop(0, count // unroll, step, 0)
    peak = jnp.max(tops[...], axis=1, keepdims=True)
    shrink = jnp.exp2(tops[...] - peak)
    total = jnp.sum(sums[...] * shrink, axis=1, keepdims=True)
    mixed = jnp.sum(cross[...] * shrink[rows:, :], axis=1, keepdims=True)
    lane = lax.broadcasted_iota(jnp.int32, (rows, LANES), 1)
    table = jnp.where(lane == 0, peak[0:rows], 0.0)
    table = jnp.where(lane == 1, total[0:rows], table)
    table = jnp.where(lane == 2, peak[rows:], table)
    table = jnp.where(lane == 3, total[rows:], table)
    table = jnp.where(lane == 4, mixed, table)
    if done:
        stats[:, 0:rows] = done[0][...]
        stats[:, rows:] = table.T[0:8, :]
    else:
        stats[...] = table.T[0:8, :]


def back_kernel(devices, factor, block, parts, which, unroll, *refs):
    stat_refs, (logits, protos, center) = refs[:devices], refs[devices : devices + 3]
    outs = refs[devices + 3 : devices + 3 + parts]
    loss = refs[devices + 3 + parts]
    total, *grads = refs[devices + 4 + parts :]
    rows = logits.shape[0] // 2
    each = rows // parts
    slots = range(which * parts, (which + 1) * parts)
    stats = [
        jnp.concatenate([ref[:, (j ^ k) * each : ((j ^ k) + 1) * each] for j in slots], axis=1)
        for k, ref in enumerate(stat_refs)
    ]
    peak_s = functools.reduce(jnp.maximum, [x[0:1] for x in stats])
    peak_t = functools.reduce(jnp.maximum, [x[2:3] for x in stats])
    sum_s = sum(x[1:2] * jnp.exp2(x[0:1] - peak_s) for x in stats)
    sum_t = sum(x[3:4] * jnp.exp2(x[2:3] - peak_t) for x in stats)
    cross = sum(x[4:5] * jnp.exp2(x[2:3] - peak_t) for x in stats)
    row_loss = LN2 * peak_s + jnp.log(sum_s) - LN2 * (cross / sum_t)
    loss[...] = jnp.broadcast_to(jnp.sum(row_loss, axis=1, keepdims=True), loss.shape)

    def columns(row):
        return jnp.broadcast_to(row, (LANES, rows)).T

    top_s = columns(peak_s + jnp.log2(sum_s * (1.0 / factor)))
    top_t = columns(peak_t + jnp.log2(sum_t * (1.0 / factor)))
    total[...] = jnp.zeros(total.shape, F32)
    groups = block // LANES
    chunk = 16

    def scale(base, u):
        lanes = [pl.ds(base + u * block + g * LANES, LANES) for g in range(groups)]
        for g, lane in enumerate(lanes):
            offset = center[:, lane] * SCALE_T
            for start in range(0, rows, chunk):
                srow = slice(start, start + chunk)
                trow = slice(rows + start, rows + start + chunk)
                value = jnp.exp2(logits[srow, lane] * SCALE_S - top_s[srow])
                value = value - jnp.exp2(logits[trow, lane] * SCALE_T - offset - top_t[srow])
                grads[u][srow, g * LANES : (g + 1) * LANES] = value.astype(BF16)

    def step(index, carry):
        base = pl.multiple_of(index * (unroll * block), unroll * block)
        for u in range(unroll):
            scale(base, u)
            total[...] += dot(grads[u][...], protos[pl.ds(base + u * block, block), :])
        return carry

    lax.fori_loop(0, protos.shape[0] // (block * unroll), step, 0)
    for part in range(parts):
        outs[part][...] = total[part * each : (part + 1) * each, :].astype(outs[part].dtype)


def direction_kernel(devices, halves, *refs):
    backs, (unit, radius), losses, (out,) = (
        refs[:devices],
        refs[devices : devices + 2],
        refs[devices + 2 : devices + 2 + halves],
        refs[devices + 2 + halves :],
    )
    rows = unit.shape[0]
    back = sum(ref[...].astype(F32) for ref in backs)
    inner = jnp.sum(unit[...] * back, axis=1, keepdims=True)
    out[0:rows, :] = ((back - unit[...] * inner) / radius[:, 0:1]).astype(BF16)
    value = jnp.broadcast_to(sum(ref[0:1, 0:1] for ref in losses), (16, out.shape[1]))
    high = value.astype(BF16).astype(F32)
    middle = (value - high).astype(BF16).astype(F32)
    low = value - high - middle
    row = lax.broadcasted_iota(jnp.int32, value.shape, 0)
    out[rows:, :] = jnp.where(row == 0, high, jnp.where(row == 1, middle, low)).astype(BF16)


def hidden_kernel(direction, weight, out):
    rows = out.shape[0]
    out[...] = dot(direction[0:rows, :], weight[...], NT).astype(BF16)


def head_kernel(dp, proto, total_rows, *refs):
    cols, dirs = refs[:dp], refs[dp : 2 * dp]
    outs = refs[2 * dp : 2 * dp + proto]
    loss = refs[2 * dp + proto]
    left, right, result = refs[2 * dp + proto + 1 :]
    rows = cols[0].shape[0]
    value = jnp.zeros((1, LANES), F32)
    for k in range(dp):
        left[k * rows : (k + 1) * rows, :] = cols[k][...]
        right[k * rows : (k + 1) * rows, :] = dirs[k][0:rows, :]
        for term in range(3):
            value = value + dirs[k][rows + term : rows + term + 1, 0:LANES].astype(F32)
    loss[...] = jnp.broadcast_to(value * (1.0 / total_rows), loss.shape)
    result[...] = dot(left[...], right[...], TN)
    me = lax.axis_index("proto")
    size = outs[0].shape[0]
    for k in range(proto):
        first = pl.multiple_of(jnp.bitwise_xor(me, k) * size, 8)
        outs[k][...] = result[pl.ds(first, size), :].astype(outs[k].dtype)


def exchange(x, axis, k):
    size = lax.axis_size(axis)
    return lax.ppermute(x, axis, [(i, i ^ k) for i in range(size)])


def per_device(hidden_states, teacher_feats, masks, head_weight, prototypes, center):
    dp, proto = lax.axis_size("dp"), lax.axis_size("proto")
    assert dp & (dp - 1) == 0 and proto & (proto - 1) == 0
    hid, bot = head_weight.shape
    rows = masks.shape[0] * masks.shape[1]
    local = prototypes.shape[0]
    total_rows = rows * dp * proto
    factor = LOSS_SCALE / (total_rows * STUDENT_TEMP)
    width = hid // dp
    half = proto // 2
    count = half * rows
    block = math.gcd(local, max(LANES, 2**17 // count))
    steps = local // block
    unroll = math.gcd(steps, 6)

    pick = pl.pallas_call(
        functools.partial(pick_kernel, dp),
        out_shape=shapes(
            ((2 * rows, bot), BF16), ((rows, bot), F32), ((rows, LANES), F32),
            *[((rows, width), BF16)] * dp,
        ),
        in_specs=[HBM] * 4,
        out_specs=(VMEM,) * (3 + dp),
        scratch_shapes=[
            pltpu.VMEM(hidden_states.shape, BF16),
            pltpu.VMEM(teacher_feats.shape, BF16),
            pltpu.VMEM(masks.shape, jnp.int32),
            pltpu.VMEM(head_weight.shape, BF16),
            pltpu.VMEM((rows, hid), BF16),
            pltpu.SemaphoreType.DMA((3 + masks.shape[0],)),
        ],
        compiler_params=params(16),
        cost_estimate=cost(2 * rows * hid * bot, hidden_states.size * 2),
        name="pick",
    )(*[pltpu.with_memory_space_constraint(x, pltpu.HBM) for x in (hidden_states, teacher_feats, masks, head_weight)])
    own, unit, radius = pick[:3]
    near = [own] + [exchange(own, "proto", k) for k in range(1, proto)]
    cols = [pick[3]] + [exchange(pick[3 + k], "dp", k) for k in range(1, dp)]

    offsets = center.reshape(1, local)

    def stats_call(parts, table, fetch, *done):
        return pl.pallas_call(
            functools.partial(stats_kernel, half, block, unroll, fetch),
            out_shape=(
                pltpu.VMEM((2 * count, local), F32),
                jax.ShapeDtypeStruct((8, count if fetch else 2 * count), F32),
            ) + ((pltpu.VMEM((local, bot), BF16),) if fetch else ()),
            in_specs=[VMEM] * half + [HBM if fetch else VMEM, VMEM] + [VMEM] * len(done),
            out_specs=(VMEM,) * (3 if fetch else 2),
            scratch_shapes=([pltpu.SemaphoreType.DMA((steps,))] if fetch else []) + [
                pltpu.VMEM((2 * count, bot), BF16),
                pltpu.VMEM((2 * count, LANES), F32),
                pltpu.VMEM((2 * count, LANES), F32),
                pltpu.VMEM((count, LANES), F32),
            ],
            compiler_params=params(6),
            cost_estimate=cost(4 * count * local * bot * 2, local * bot * 2),
            name="stats",
        )(*parts, table, offsets, *done)

    first, sums, table = stats_call(near[:half], pltpu.with_memory_space_constraint(prototypes, pltpu.HBM), True)
    second, mine = stats_call(near[half:], table, False, sums)
    others = [mine] + [exchange(mine, "proto", k) for k in range(1, proto)]

    def back_call(which):
        kinds = [F32] * half
        return pl.pallas_call(
            functools.partial(back_kernel, proto, factor, block, half, which, unroll),
            out_shape=shapes(*[((rows, bot), kind) for kind in kinds], ((8, LANES), F32)),
            in_specs=[VMEM] * (proto + 3),
            out_specs=(VMEM,) * (half + 1),
            scratch_shapes=[pltpu.VMEM((count, bot), F32)] + [pltpu.VMEM((count, block), BF16)] * unroll,
            compiler_params=params(6),
            cost_estimate=cost(2 * count * local * bot * 2, local * bot * 2),
            name="back",
        )(*others, (first, second)[which], table, offsets)

    far = back_call(1)
    close = back_call(0)
    parts = list(close[:half]) + list(far[:half])
    backs = [parts[0]] + [exchange(parts[k], "proto", k) for k in range(1, proto)]

    direction = pl.pallas_call(
        functools.partial(direction_kernel, proto, 2),
        out_shape=jax.ShapeDtypeStruct((rows + 16, bot), BF16),
        in_specs=[VMEM] * (proto + 4),
        out_specs=VMEM,
        compiler_params=params(4),
        cost_estimate=cost(rows * bot * 16, rows * bot * 16),
        name="direction",
    )(*backs, unit, radius, close[half], far[half])
    dirs = [direction] + [exchange(direction, "dp", k) for k in range(1, dp)]
    grad_hidden = pl.pallas_call(
        hidden_kernel,
        out_shape=jax.ShapeDtypeStruct((rows, hid), BF16),
        in_specs=[VMEM] * 2,
        out_specs=VMEM,
        compiler_params=params(8),
        cost_estimate=cost(2 * rows * hid * bot, hid * bot * 2),
        name="hidden",
    )(direction, head_weight)

    size = width // proto
    head = pl.pallas_call(
        functools.partial(head_kernel, dp, proto, total_rows),
        out_shape=shapes(
            *[((size, bot), F32 if k == 0 else BF16) for k in range(proto)], ((8, LANES), F32)
        ),
        in_specs=[VMEM] * (2 * dp),
        out_specs=(VMEM,) * (proto + 1),
        scratch_shapes=[
            pltpu.VMEM((dp * rows, width), BF16),
            pltpu.VMEM((dp * rows, bot), BF16),
            pltpu.VMEM((width, bot), F32),
        ],
        compiler_params=params(8),
        cost_estimate=cost(2 * dp * rows * width * bot, dp * rows * bot * 2),
        name="head",
    )(*cols, *dirs)
    grad_head = head[0]
    for k in range(1, proto):
        grad_head = grad_head + exchange(head[k], "proto", k).astype(F32)
    return (head[proto][0, 0], grad_hidden, grad_head)


def solution(mesh):
    return jax.shard_map(
        per_device,
        mesh=mesh,
        in_specs=(
            P(("dp", "proto"), None, None),
            P(("dp", "proto"), None, None),
            P(("dp", "proto"), None),
            P(),
            P("proto", None),
            P("proto"),
        ),
        out_specs=(P(), P(("dp", "proto"), None), P(("dp", "proto"), None)),
        check_vma=False,
    )
```

time: 315 us -> 78.5 us (0.25)
  matrix products: 103 us -> 0 us
  waiting for transfers between devices: 106 us -> 14.8 us
  blocking collectives: 62 us -> 0 us
  starting transfers between devices: 0.08 us -> 31.3 us
  Pallas kernels: 0 us -> 29.5 us
  local copies, waits for them, and re-layouts: 17 us -> 1.31 us
  between operations: 15.9 us -> 0.72 us
  other arithmetic: 8.1 us -> 0.67 us
    reduce_scatter x2 -> x0, waiting for transfers between devices: 106 us -> none  [the longest x1 85.6 us: per_device(): lax.psum_scatter(lax.dot_general(picked, direction, (((0,), (0,)), ((), (...]
    dot_general x35 -> x0, matrix products: 103 us -> none  [the longest x16 48.5 us: block_logits(): lax.dot_general(teacher, tile, dims, preferred_element_type=jnp.float32)]
    ppermute x0 -> x26, starting transfers between devices: none -> 31.3 us  [exchange(): return lax.ppermute(x, axis, [(i, i ^ k) for i in range(size)])]
    pallas_call x0 -> x8, Pallas kernels: none -> 29.5 us  [the longest x2 17.5 us: stats_call(): pl.pallas_call(functools.partial(stats_kernel, half, block, unroll, fetch...]
    all_gather x2 -> x0, blocking collectives: 29.5 us -> none  [the longest x1 15.5 us: per_device(): lax.all_gather(student, 'proto', axis=0, tiled=True)]
    psum x2 -> x0, blocking collectives: 20.8 us -> none  [the longest x1 12.4 us: per_device(): loss = lax.psum(jnp.sum(row_loss), 'dp') / total_rows]
    ppermute x0 -> x26, waiting for transfers between devices: none -> 14.8 us  [exchange(): return lax.ppermute(x, axis, [(i, i ^ k) for i in range(size)])]
    dynamic_slice x16 -> x0, local copies, waits for them, and re-layouts: 12.6 us -> none  [block_logits(): offset = lax.dynamic_slice_in_dim(center, first, width, 0)]
  transfers between devices with their start and end apart: 2 -> 26, of which waited for: 2 -> 12; matrix products, arithmetic and copies ran while one was open for 1% -> 1% of each run, Pallas kernels for 0% -> 20%
where the time goes in v1:
time: 78.5 us; the launch traced here: 78.3 us
  starting transfers between devices  31.3 us (40%)
  Pallas kernels  29.5 us (38%)
  waiting for transfers between devices  14.8 us (19%)
  local copies, waits for them, and re-layouts  1.31 us (2%)
    ppermute x26, starting transfers between devices, exchange(): return lax.ppermute(x, axis, [(i, i ^ k) for i in range(size)])  31.3 us
    pallas_call x2, Pallas kernels, stats_call(): pl.pallas_call(functools.partial(stats_kernel, half, block, unroll, fetch...  17.5 us
    ppermute x26, waiting for transfers between devices, exchange(): return lax.ppermute(x, axis, [(i, i ^ k) for i in range(size)])  14.8 us
    pallas_call x2, Pallas kernels, back_call(): pl.pallas_call(functools.partial(back_kernel, proto, factor, block, half,...  7.37 us
    pallas_call x1, Pallas kernels, per_device(): pl.pallas_call(functools.partial(pick_kernel, dp), out_shape=shapes(((2 *...  2.84 us
  transfers between devices with their start and end apart: 26, of which 12 were waited for; matrix products, arithmetic and copies ran while one was open for 1% of the time, Pallas kernels for 20%

profile of v1, /device:TPU:0, one launch (start us, length us, event | category | flops | bytes accessed | tf_op | source)
XLA Modules:
  0.0 78.3 jit_solution(5709574963271332257)
XLA Ops:
  0.6 2.8 %pick.1 = (bf16[128,384]{1,0:T(8,128)(2,1)S(1)}, f32[64,384]{1,0:T(8,128)S(1)}, f32[64,128]{1,0:T(8,128)S(1)}, bf16[64,256]{1,0:T(8,128)(2,1)S(1)}, bf16[64,256]...) custom-call(bf16[2,256,2048]{2,1,0:T(8,128)(2,1)} %hidden_hbm.1, ...), custom_call_target="tpu_custom_call" | custom-call | flops 100663296 | bytes 2097152 | tf_op jit(solution)/shard_map/pick/pallas_call | solution.py:284
  3.5 3.1 %collective-permute-start.9 = (bf16[128,384]{1,0:T(8,128)(2,1)S(1)}, bf16[128,384]{1,0:T(8,128)(2,1)S(1)}, u32[]{:S(2)}, u32[]{:S(2)}) collective-permute-start(bf16[128,384]{1,0:T(8,128)(2,1)S(1)} %get-tuple-element.38.refs_0_), channel_id=1, source_target_pairs={{0,1},{1,0},{2,3},{3,2},{4,5},{5,4},{6,7},{7,6},{8,9},{9,8},{10,11... | collective-permute-start | bytes 294920 | tf_op jit(solution)/shard_map/ppermute | solution.py:266
  6.6 2.5 %collective-permute-start.8 = (bf16[128,384]{1,0:T(8,128)(2,1)S(1)}, bf16[128,384]{1,0:T(8,128)(2,1)S(1)}, u32[]{:S(2)}, u32[]{:S(2)}) collective-permute-start(bf16[128,384]{1,0:T(8,128)(2,1)S(1)} %get-tuple-element.38.refs_0_), channel_id=1, source_target_pairs={{0,3},{1,2},{2,1},{3,0},{4,7},{5,6},{6,5},{7,4},{8,11},{9,10},{10,... | collective-permute-start | bytes 294920 | tf_op jit(solution)/shard_map/ppermute | solution.py:266
  9.1 0.1 collective-permute-start.7
  9.2 0.2 collective-permute-done.9.refs_1_
  9.4 0.8 %copy-done.1 = f32[12288]{0:T(1024)S(1)} copy-done((f32[12288]{0:T(1024)S(1)}, f32[12288]{0:T(1024)}, u32[]{:S(2)}) %copy-start.1) | copy-done | bytes 49176
  10.2 10.4 %stats.2 = (f32[256,12288]{1,0:T(8,128)S(1)}, f32[8,128]{1,0:T(8,128)S(1)}, bf16[12288,384]{1,0:T(8,128)(2,1)S(1)}) custom-call(bf16[128,384]{1,0:T(8,128)(2,1)S(1)} %get-tuple-element.38.refs_0_, bf16[128,384]{1,0:T(8,128)(2,1)S(1)} %collective-permute-done.9.refs_1_, bf16[12288,384]{1,0:T(8,128)(2,1)} %refs_2_.1, f32[1,12288]{1,0:T(1,128)S(1)} %bitcast.2), custom_call_target="tpu_custom_call" | custom-call | flops 4831838208 | bytes 9437184 | tf_op jit(solution)/shard_map/stats/pallas_call | solution.py:311
  20.6 0.0 collective-permute-done.7.refs_0_
  20.7 7.0 %stats.3 = (f32[256,12288]{1,0:T(8,128)S(1)}, f32[8,256]{1,0:T(8,128)S(1)}) custom-call(bf16[128,384]{1,0:T(8,128)(2,1)S(1)} %collective-permute-done.7.refs_0_, bf16[128,384]{1,0:T(8,128)(2,1)S(1)} %collective-permute-done.8.refs_1_, bf16[12288,384]{1,0:T(8,128)(2,1)S(1)} %get-tuple-element.39.refs_2_.refs_5_, f32[1,12288]{1,0:T(1,128)S(1)} %bitcast.3, ...), custom_call_target="tpu_custom_call" | custom-call | flops 4831838208 | bytes 9437184 | tf_op jit(solution)/shard_map/stats/pallas_call | solution.py:311
  27.7 4.9 %collective-permute-start.12 = (f32[8,256]{1,0:T(8,128)S(1)}, f32[8,256]{1,0:T(8,128)S(1)}, u32[]{:S(2)}, u32[]{:S(2)}) collective-permute-start(f32[8,256]{1,0:T(8,128)S(1)} %get-tuple-element.41.refs_0_), channel_id=1, source_target_pairs={{0,3},{1,2},{2,1},{3,0},{4,7},{5,6},{6,5},{7,4},{8,11},{9,10},{10,... | collective-permute-start | bytes 24584 | tf_op jit(solution)/shard_map/ppermute | solution.py:266
  32.6 0.6 collective-permute-start.10
  33.3 1.0 %collective-permute-done.12.refs_3_ = f32[8,256]{1,0:T(8,128)S(1)} collective-permute-done((f32[8,256]{1,0:T(8,128)S(1)}, f32[8,256]{1,0:T(8,128)S(1)}, u32[]{:S(2)}, u32[]{:S(2)}) %collective-permute-start.12) | collective-permute-done | bytes 8224 | tf_op jit(solution)/shard_map/ppermute | solution.py:266
  34.2 2.9 %collective-permute-done.11.refs_2_ = f32[8,256]{1,0:T(8,128)S(1)} collective-permute-done((f32[8,256]{1,0:T(8,128)S(1)}, f32[8,256]{1,0:T(8,128)S(1)}, u32[]{:S(2)}, u32[]{:S(2)}) %collective-permute-start.11) | collective-permute-done | bytes 8224 | tf_op jit(solution)/shard_map/ppermute | solution.py:266
  37.2 3.7 %back.3 = (f32[64,384]{1,0:T(8,128)S(1)}, f32[64,384]{1,0:T(8,128)S(1)}, f32[8,128]{1,0:T(8,128)S(1)}) custom-call(f32[8,256]{1,0:T(8,128)S(1)} %get-tuple-element.41.refs_0_, f32[8,256]{1,0:T(8,128)S(1)} %collective-permute-done.10.refs_1_, f32[8,256]{1,0:T(8,128)S(1)} %collective-permute-done.11.refs_2_, f32[8,256]{1,0:T(8,128)S(1)} %collective-permute-done.12.refs_3_, ...), custom_call_target="tpu_custom_call" | custom-call | flops 2415919104 | bytes 9437184 | tf_op jit(solution)/shard_map/back/pallas_call | solution.py:336
  40.9 2.1 %collective-permute-start.14 = (f32[64,384]{1,0:T(8,128)S(1)}, f32[64,384]{1,0:T(8,128)S(1)}, u32[]{:S(2)}, u32[]{:S(2)}) collective-permute-start(f32[64,384]{1,0:T(8,128)S(1)} %get-tuple-element.46), channel_id=1, source_target_pairs={{0,2},{1,3},{2,0},{3,1},{4,6},{5,7},{6,4},{7,5},{8,10},{9,11},{10,... | collective-permute-start | bytes 294920 | tf_op jit(solution)/shard_map/ppermute | solution.py:266
  42.9 0.1 collective-permute-start.15
  43.0 3.7 %back.2 = (f32[64,384]{1,0:T(8,128)S(1)}, f32[64,384]{1,0:T(8,128)S(1)}, f32[8,128]{1,0:T(8,128)S(1)}) custom-call(f32[8,256]{1,0:T(8,128)S(1)} %get-tuple-element.41.refs_0_, f32[8,256]{1,0:T(8,128)S(1)} %collective-permute-done.10.refs_1_, f32[8,256]{1,0:T(8,128)S(1)} %collective-permute-done.11.refs_2_, f32[8,256]{1,0:T(8,128)S(1)} %collective-permute-done.12.refs_3_, ...), custom_call_target="tpu_custom_call" | custom-call | flops 2415919104 | bytes 9437184 | tf_op jit(solution)/shard_map/back/pallas_call | solution.py:336
  46.7 1.5 %collective-permute-start.13 = (f32[64,384]{1,0:T(8,128)S(1)}, f32[64,384]{1,0:T(8,128)S(1)}, u32[]{:S(2)}, u32[]{:S(2)}) collective-permute-start(f32[64,384]{1,0:T(8,128)S(1)} %get-tuple-element.44), channel_id=1, source_target_pairs={{0,1},{1,0},{2,3},{3,2},{4,5},{5,4},{6,7},{7,6},{8,9},{9,8},{10,11... | collective-permute-start | bytes 294920 | tf_op jit(solution)/shard_map/ppermute | solution.py:266
  48.2 1.5 %collective-permute-start.1 = (bf16[64,256]{1,0:T(8,128)(2,1)S(1)}, bf16[64,256]{1,0:T(8,128)(2,1)S(1)}, u32[]{:S(2)}, u32[]{:S(2)}) collective-permute-start(bf16[64,256]{1,0:T(8,128)(2,1)S(1)} %get-tuple-element.32), channel_id=1, source_target_pairs={{0,8},{4,12},{8,0},{12,4},{16,24},{20,28},{24,16},{28,20},{1,9},{5... | collective-permute-start | bytes 98312 | tf_op jit(solution)/shard_map/ppermute | solution.py:266
  49.7 0.4 collective-permute-start.2
  50.0 1.5 %collective-permute-start.3 = (bf16[64,256]{1,0:T(8,128)(2,1)S(1)}, bf16[64,256]{1,0:T(8,128)(2,1)S(1)}, u32[]{:S(2)}, u32[]{:S(2)}) collective-permute-start(bf16[64,256]{1,0:T(8,128)(2,1)S(1)} %get-tuple-element.34), channel_id=1, source_target_pairs={{0,16},{4,20},{8,24},{12,28},{16,0},{20,4},{24,8},{28,12},{1,17},{... | collective-permute-start | bytes 98312 | tf_op jit(solution)/shard_map/ppermute | solution.py:266
  51.6 0.1 direction.1.refs_8_
  51.7 1.1 %collective-permute-start.22 = (bf16[80,384]{1,0:T(8,128)(2,1)S(1)}, bf16[80,384]{1,0:T(8,128)(2,1)S(1)}, u32[]{:S(2)}, u32[]{:S(2)}) collective-permute-start(bf16[80,384]{1,0:T(8,128)(2,1)S(1)} %direction.1.refs_8_), channel_id=1, source_target_pairs={{0,28},{4,24},{8,20},{12,16},{16,12},{20,8},{24,4},{28,0},{1,29},{... | collective-permute-start | bytes 184328 | tf_op jit(solution)/shard_map/ppermute | solution.py:266
  52.8 1.5 %collective-permute-start.21 = (bf16[80,384]{1,0:T(8,128)(2,1)S(1)}, bf16[80,384]{1,0:T(8,128)(2,1)S(1)}, u32[]{:S(2)}, u32[]{:S(2)}) collective-permute-start(bf16[80,384]{1,0:T(8,128)(2,1)S(1)} %direction.1.refs_8_), channel_id=1, source_target_pairs={{0,24},{4,28},{8,16},{12,20},{16,8},{20,12},{24,0},{28,4},{1,25},{... | collective-permute-start | bytes 184328 | tf_op jit(solution)/shard_map/ppermute | solution.py:266
  54.3 1.2 %collective-permute-start.4 = (bf16[64,256]{1,0:T(8,128)(2,1)S(1)}, bf16[64,256]{1,0:T(8,128)(2,1)S(1)}, u32[]{:S(2)}, u32[]{:S(2)}) collective-permute-start(bf16[64,256]{1,0:T(8,128)(2,1)S(1)} %get-tuple-element.35), channel_id=1, source_target_pairs={{0,20},{4,16},{8,28},{12,24},{16,4},{20,0},{24,12},{28,8},{1,21},{... | collective-permute-start | bytes 98312 | tf_op jit(solution)/shard_map/ppermute | solution.py:266
  55.5 1.6 %collective-permute-start.5 = (bf16[64,256]{1,0:T(8,128)(2,1)S(1)}, bf16[64,256]{1,0:T(8,128)(2,1)S(1)}, u32[]{:S(2)}, u32[]{:S(2)}) collective-permute-start(bf16[64,256]{1,0:T(8,128)(2,1)S(1)} %get-tuple-element.36), channel_id=1, source_target_pairs={{0,24},{4,28},{8,16},{12,20},{16,8},{20,12},{24,0},{28,4},{1,25},{... | collective-permute-start | bytes 98312 | tf_op jit(solution)/shard_map/ppermute | solution.py:266
  57.1 0.1 collective-permute-start.6
  57.2 2.4 %collective-permute-done.4.refs_5_ = bf16[64,256]{1,0:T(8,128)(2,1)S(1)} collective-permute-done((bf16[64,256]{1,0:T(8,128)(2,1)S(1)}, bf16[64,256]{1,0:T(8,128)(2,1)S(1)}, u32[]{:S(2)}, u32[]{:S(2)}) %collective-permute-start.4) | collective-permute-done | bytes 32800 | tf_op jit(solution)/shard_map/ppermute | solution.py:266
  59.6 0.2 collective-permute-start.20
  59.8 0.5 collective-permute-done.5.refs_6_
  60.3 1.0 %collective-permute-start.19 = (bf16[80,384]{1,0:T(8,128)(2,1)S(1)}, bf16[80,384]{1,0:T(8,128)(2,1)S(1)}, u32[]{:S(2)}, u32[]{:S(2)}) collective-permute-start(bf16[80,384]{1,0:T(8,128)(2,1)S(1)} %direction.1.refs_8_), channel_id=1, source_target_pairs={{0,16},{4,20},{8,24},{12,28},{16,0},{20,4},{24,8},{28,12},{1,17},{... | collective-permute-start | bytes 184328 | tf_op jit(solution)/shard_map/ppermute | solution.py:266
  61.4 0.2 collective-permute-done.6.refs_7_
  61.5 0.8 collective-permute-start.18
  62.3 1.0 %collective-permute-start.17 = (bf16[80,384]{1,0:T(8,128)(2,1)S(1)}, bf16[80,384]{1,0:T(8,128)(2,1)S(1)}, u32[]{:S(2)}, u32[]{:S(2)}) collective-permute-start(bf16[80,384]{1,0:T(8,128)(2,1)S(1)} %direction.1.refs_8_), channel_id=1, source_target_pairs={{0,8},{4,12},{8,0},{12,4},{16,24},{20,28},{24,16},{28,20},{1,9},{5... | collective-permute-start | bytes 184328 | tf_op jit(solution)/shard_map/ppermute | solution.py:266
  63.3 0.1 collective-permute-start.16
  63.4 0.2 collective-permute-done.20.refs_13_
  63.6 1.6 %collective-permute-done.19.refs_12_ = bf16[80,384]{1,0:T(8,128)(2,1)S(1)} collective-permute-done((bf16[80,384]{1,0:T(8,128)(2,1)S(1)}, bf16[80,384]{1,0:T(8,128)(2,1)S(1)}, u32[]{:S(2)}, u32[]{:S(2)}) %collective-permute-start.19) | collective-permute-done | bytes 61472 | tf_op jit(solution)/shard_map/ppermute | solution.py:266
  65.2 0.3 collective-permute-done.18.refs_11_
  65.5 1.6 %collective-permute-done.17.refs_10_ = bf16[80,384]{1,0:T(8,128)(2,1)S(1)} collective-permute-done((bf16[80,384]{1,0:T(8,128)(2,1)S(1)}, bf16[80,384]{1,0:T(8,128)(2,1)S(1)}, u32[]{:S(2)}, u32[]{:S(2)}) %collective-permute-start.17) | collective-permute-done | bytes 61472 | tf_op jit(solution)/shard_map/ppermute | solution.py:266
  67.1 0.4 head.1
  67.5 1.3 %collective-permute-start.23 = (bf16[64,384]{1,0:T(8,128)(2,1)S(1)}, bf16[64,384]{1,0:T(8,128)(2,1)S(1)}, u32[]{:S(2)}, u32[]{:S(2)}) collective-permute-start(bf16[64,384]{1,0:T(8,128)(2,1)S(1)} %get-tuple-element.54), channel_id=1, source_target_pairs={{0,1},{1,0},{2,3},{3,2},{4,5},{5,4},{6,7},{7,6},{8,9},{9,8},{10,11... | collective-permute-start | bytes 147464 | tf_op jit(solution)/shard_map/ppermute | solution.py:266
  68.9 2.9 %collective-permute-start.24 = (bf16[64,384]{1,0:T(8,128)(2,1)S(1)}, bf16[64,384]{1,0:T(8,128)(2,1)S(1)}, u32[]{:S(2)}, u32[]{:S(2)}) collective-permute-start(bf16[64,384]{1,0:T(8,128)(2,1)S(1)} %get-tuple-element.55), channel_id=1, source_target_pairs={{0,2},{1,3},{2,0},{3,1},{4,6},{5,7},{6,4},{7,5},{8,10},{9,11},{10,... | collective-permute-start | bytes 147464 | tf_op jit(solution)/shard_map/ppermute | solution.py:266
  71.8 0.2 collective-permute-start.25
  72.0 1.3 %hidden.1 = bf16[64,2048]{1,0:T(8,128)(2,1)} custom-call(bf16[80,384]{1,0:T(8,128)(2,1)S(1)} %direction.1.refs_8_, bf16[2048,384]{1,0:T(8,128)(2,1)S(1)} %copy-done), custom_call_target="tpu_custom_call" | custom-call | flops 100663296 | bytes 1572864 | tf_op jit(solution)/shard_map/hidden/pallas_call | solution.py:362
  73.3 0.5 slice.3
  73.8 0.2 collective-permute-done.24
  74.1 3.6 %collective-permute-done.25 = bf16[64,384]{1,0:T(8,128)(2,1)S(1)} collective-permute-done((bf16[64,384]{1,0:T(8,128)(2,1)S(1)}, bf16[64,384]{1,0:T(8,128)(2,1)S(1)}, u32[]{:S(2)}, u32[]{:S(2)}) %collective-permute-start.25) | collective-permute-done | bytes 49184 | tf_op jit(solution)/shard_map/ppermute | solution.py:266
  77.7 0.7 convert_add_fusion
  (18 shorter events, 0.0 us)
Async XLA Ops:
  3.5 5.9 %collective-permute-start.9 = (bf16[128,384]{1,0:T(8,128)(2,1)S(1)}, bf16[128,384]{1,0:T(8,128)(2,1)S(1)}, u32[]{:S(2)}, u32[]{:S(2)}) collective-permute-start(bf16[128,384]{1,0:T(8,128)(2,1)S(1)} %get-tuple-element.38.refs_0_), channel_id=1, source_target_pairs={{0,1},{1,0},{2,3},{3,2},{4,5},{5,4},{6,7},{7,6},{8,9},{9,8},{10,11... | collective-permute-start | bytes 294920 | tf_op jit(solution)/shard_map/ppermute | solution.py:266
  6.6 14.0 %collective-permute-start.8 = (bf16[128,384]{1,0:T(8,128)(2,1)S(1)}, bf16[128,384]{1,0:T(8,128)(2,1)S(1)}, u32[]{:S(2)}, u32[]{:S(2)}) collective-permute-start(bf16[128,384]{1,0:T(8,128)(2,1)S(1)} %get-tuple-element.38.refs_0_), channel_id=1, source_target_pairs={{0,3},{1,2},{2,1},{3,0},{4,7},{5,6},{6,5},{7,4},{8,11},{9,10},{10,... | collective-permute-start | bytes 294920 | tf_op jit(solution)/shard_map/ppermute | solution.py:266
  9.1 11.6 %collective-permute-start.7 = (bf16[128,384]{1,0:T(8,128)(2,1)S(1)}, bf16[128,384]{1,0:T(8,128)(2,1)S(1)}, u32[]{:S(2)}, u32[]{:S(2)}) collective-permute-start(bf16[128,384]{1,0:T(8,128)(2,1)S(1)} %get-tuple-element.38.refs_0_), channel_id=1, source_target_pairs={{0,2},{1,3},{2,0},{3,1},{4,6},{5,7},{6,4},{7,5},{8,10},{9,11},{10,... | collective-permute-start | bytes 294920 | tf_op jit(solution)/shard_map/ppermute | solution.py:266
  9.4 0.8 %copy-start.1 = (f32[12288]{0:T(1024)S(1)}, f32[12288]{0:T(1024)}, u32[]{:S(2)}) copy-start(f32[12288]{0:T(1024)} %param.11) | copy-start | bytes 147460
  27.7 6.6 %collective-permute-start.12 = (f32[8,256]{1,0:T(8,128)S(1)}, f32[8,256]{1,0:T(8,128)S(1)}, u32[]{:S(2)}, u32[]{:S(2)}) collective-permute-start(f32[8,256]{1,0:T(8,128)S(1)} %get-tuple-element.41.refs_0_), channel_id=1, source_target_pairs={{0,3},{1,2},{2,1},{3,0},{4,7},{5,6},{6,5},{7,4},{8,11},{9,10},{10,... | collective-permute-start | bytes 24584 | tf_op jit(solution)/shard_map/ppermute | solution.py:266
  32.6 4.5 %collective-permute-start.11 = (f32[8,256]{1,0:T(8,128)S(1)}, f32[8,256]{1,0:T(8,128)S(1)}, u32[]{:S(2)}, u32[]{:S(2)}) collective-permute-start(f32[8,256]{1,0:T(8,128)S(1)} %get-tuple-element.41.refs_0_), channel_id=1, source_target_pairs={{0,2},{1,3},{2,0},{3,1},{4,6},{5,7},{6,4},{7,5},{8,10},{9,11},{10,... | collective-permute-start | bytes 24584 | tf_op jit(solution)/shard_map/ppermute | solution.py:266
  32.6 4.5 %collective-permute-start.10 = (f32[8,256]{1,0:T(8,128)S(1)}, f32[8,256]{1,0:T(8,128)S(1)}, u32[]{:S(2)}, u32[]{:S(2)}) collective-permute-start(f32[8,256]{1,0:T(8,128)S(1)} %get-tuple-element.41.refs_0_), channel_id=1, source_target_pairs={{0,1},{1,0},{2,3},{3,2},{4,5},{5,4},{6,7},{7,6},{8,9},{9,8},{10,11... | collective-permute-start | bytes 24584 | tf_op jit(solution)/shard_map/ppermute | solution.py:266
  40.9 8.8 %collective-permute-start.14 = (f32[64,384]{1,0:T(8,128)S(1)}, f32[64,384]{1,0:T(8,128)S(1)}, u32[]{:S(2)}, u32[]{:S(2)}) collective-permute-start(f32[64,384]{1,0:T(8,128)S(1)} %get-tuple-element.46), channel_id=1, source_target_pairs={{0,2},{1,3},{2,0},{3,1},{4,6},{5,7},{6,4},{7,5},{8,10},{9,11},{10,... | collective-permute-start | bytes 294920 | tf_op jit(solution)/shard_map/ppermute | solution.py:266
  42.9 7.1 %collective-permute-start.15 = (f32[64,384]{1,0:T(8,128)S(1)}, f32[64,384]{1,0:T(8,128)S(1)}, u32[]{:S(2)}, u32[]{:S(2)}) collective-permute-start(f32[64,384]{1,0:T(8,128)S(1)} %get-tuple-element.47), channel_id=1, source_target_pairs={{0,3},{1,2},{2,1},{3,0},{4,7},{5,6},{6,5},{7,4},{8,11},{9,10},{10,... | collective-permute-start | bytes 294920 | tf_op jit(solution)/shard_map/ppermute | solution.py:266
  43.0 29.0 %copy-start = (bf16[2048,384]{1,0:T(8,128)(2,1)S(1)}, bf16[2048,384]{1,0:T(8,128)(2,1)}, u32[]{:S(2)}) copy-start(bf16[2048,384]{1,0:T(8,128)(2,1)} %weight.1) | copy-start | bytes 4718596
  46.7 4.8 %collective-permute-start.13 = (f32[64,384]{1,0:T(8,128)S(1)}, f32[64,384]{1,0:T(8,128)S(1)}, u32[]{:S(2)}, u32[]{:S(2)}) collective-permute-start(f32[64,384]{1,0:T(8,128)S(1)} %get-tuple-element.44), channel_id=1, source_target_pairs={{0,1},{1,0},{2,3},{3,2},{4,5},{5,4},{6,7},{7,6},{8,9},{9,8},{10,11... | collective-permute-start | bytes 294920 | tf_op jit(solution)/shard_map/ppermute | solution.py:266
  48.2 4.6 %collective-permute-start = (bf16[64,256]{1,0:T(8,128)(2,1)S(1)}, bf16[64,256]{1,0:T(8,128)(2,1)S(1)}, u32[]{:S(2)}, u32[]{:S(2)}) collective-permute-start(bf16[64,256]{1,0:T(8,128)(2,1)S(1)} %get-tuple-element.31), channel_id=1, source_target_pairs={{0,4},{4,0},{8,12},{12,8},{16,20},{20,16},{24,28},{28,24},{1,5},{5... | collective-permute-start | bytes 98312 | tf_op jit(solution)/shard_map/ppermute | solution.py:266
  48.2 6.1 %collective-permute-start.1 = (bf16[64,256]{1,0:T(8,128)(2,1)S(1)}, bf16[64,256]{1,0:T(8,128)(2,1)S(1)}, u32[]{:S(2)}, u32[]{:S(2)}) collective-permute-start(bf16[64,256]{1,0:T(8,128)(2,1)S(1)} %get-tuple-element.32), channel_id=1, source_target_pairs={{0,8},{4,12},{8,0},{12,4},{16,24},{20,28},{24,16},{28,20},{1,9},{5... | collective-permute-start | bytes 98312 | tf_op jit(solution)/shard_map/ppermute | solution.py:266
  49.7 5.8 %collective-permute-start.2 = (bf16[64,256]{1,0:T(8,128)(2,1)S(1)}, bf16[64,256]{1,0:T(8,128)(2,1)S(1)}, u32[]{:S(2)}, u32[]{:S(2)}) collective-permute-start(bf16[64,256]{1,0:T(8,128)(2,1)S(1)} %get-tuple-element.33), channel_id=1, source_target_pairs={{0,12},{4,8},{8,4},{12,0},{16,28},{20,24},{24,20},{28,16},{1,13},{... | collective-permute-start | bytes 98312 | tf_op jit(solution)/shard_map/ppermute | solution.py:266
  50.0 7.1 %collective-permute-start.3 = (bf16[64,256]{1,0:T(8,128)(2,1)S(1)}, bf16[64,256]{1,0:T(8,128)(2,1)S(1)}, u32[]{:S(2)}, u32[]{:S(2)}) collective-permute-start(bf16[64,256]{1,0:T(8,128)(2,1)S(1)} %get-tuple-element.34), channel_id=1, source_target_pairs={{0,16},{4,20},{8,24},{12,28},{16,0},{20,4},{24,8},{28,12},{1,17},{... | collective-permute-start | bytes 98312 | tf_op jit(solution)/shard_map/ppermute | solution.py:266
  51.7 10.6 %collective-permute-start.22 = (bf16[80,384]{1,0:T(8,128)(2,1)S(1)}, bf16[80,384]{1,0:T(8,128)(2,1)S(1)}, u32[]{:S(2)}, u32[]{:S(2)}) collective-permute-start(bf16[80,384]{1,0:T(8,128)(2,1)S(1)} %direction.1.refs_8_), channel_id=1, source_target_pairs={{0,28},{4,24},{8,20},{12,16},{16,12},{20,8},{24,4},{28,0},{1,29},{... | collective-permute-start | bytes 184328 | tf_op jit(solution)/shard_map/ppermute | solution.py:266
  52.8 10.5 %collective-permute-start.21 = (bf16[80,384]{1,0:T(8,128)(2,1)S(1)}, bf16[80,384]{1,0:T(8,128)(2,1)S(1)}, u32[]{:S(2)}, u32[]{:S(2)}) collective-permute-start(bf16[80,384]{1,0:T(8,128)(2,1)S(1)} %direction.1.refs_8_), channel_id=1, source_target_pairs={{0,24},{4,28},{8,16},{12,20},{16,8},{20,12},{24,0},{28,4},{1,25},{... | collective-permute-start | bytes 184328 | tf_op jit(solution)/shard_map/ppermute | solution.py:266
  54.3 5.3 %collective-permute-start.4 = (bf16[64,256]{1,0:T(8,128)(2,1)S(1)}, bf16[64,256]{1,0:T(8,128)(2,1)S(1)}, u32[]{:S(2)}, u32[]{:S(2)}) collective-permute-start(bf16[64,256]{1,0:T(8,128)(2,1)S(1)} %get-tuple-element.35), channel_id=1, source_target_pairs={{0,20},{4,16},{8,28},{12,24},{16,4},{20,0},{24,12},{28,8},{1,21},{... | collective-permute-start | bytes 98312 | tf_op jit(solution)/shard_map/ppermute | solution.py:266
  55.5 4.8 %collective-permute-start.5 = (bf16[64,256]{1,0:T(8,128)(2,1)S(1)}, bf16[64,256]{1,0:T(8,128)(2,1)S(1)}, u32[]{:S(2)}, u32[]{:S(2)}) collective-permute-start(bf16[64,256]{1,0:T(8,128)(2,1)S(1)} %get-tuple-element.36), channel_id=1, source_target_pairs={{0,24},{4,28},{8,16},{12,20},{16,8},{20,12},{24,0},{28,4},{1,25},{... | collective-permute-start | bytes 98312 | tf_op jit(solution)/shard_map/ppermute | solution.py:266
  57.1 4.4 %collective-permute-start.6 = (bf16[64,256]{1,0:T(8,128)(2,1)S(1)}, bf16[64,256]{1,0:T(8,128)(2,1)S(1)}, u32[]{:S(2)}, u32[]{:S(2)}) collective-permute-start(bf16[64,256]{1,0:T(8,128)(2,1)S(1)} %get-tuple-element.37), channel_id=1, source_target_pairs={{0,28},{4,24},{8,20},{12,16},{16,12},{20,8},{24,4},{28,0},{1,29},{... | collective-permute-start | bytes 98312 | tf_op jit(solution)/shard_map/ppermute | solution.py:266
  59.6 4.0 %collective-permute-start.20 = (bf16[80,384]{1,0:T(8,128)(2,1)S(1)}, bf16[80,384]{1,0:T(8,128)(2,1)S(1)}, u32[]{:S(2)}, u32[]{:S(2)}) collective-permute-start(bf16[80,384]{1,0:T(8,128)(2,1)S(1)} %direction.1.refs_8_), channel_id=1, source_target_pairs={{0,20},{4,16},{8,28},{12,24},{16,4},{20,0},{24,12},{28,8},{1,21},{... | collective-permute-start | bytes 184328 | tf_op jit(solution)/shard_map/ppermute | solution.py:266
  60.3 4.9 %collective-permute-start.19 = (bf16[80,384]{1,0:T(8,128)(2,1)S(1)}, bf16[80,384]{1,0:T(8,128)(2,1)S(1)}, u32[]{:S(2)}, u32[]{:S(2)}) collective-permute-start(bf16[80,384]{1,0:T(8,128)(2,1)S(1)} %direction.1.refs_8_), channel_id=1, source_target_pairs={{0,16},{4,20},{8,24},{12,28},{16,0},{20,4},{24,8},{28,12},{1,17},{... | collective-permute-start | bytes 184328 | tf_op jit(solution)/shard_map/ppermute | solution.py:266
  61.5 4.0 %collective-permute-start.18 = (bf16[80,384]{1,0:T(8,128)(2,1)S(1)}, bf16[80,384]{1,0:T(8,128)(2,1)S(1)}, u32[]{:S(2)}, u32[]{:S(2)}) collective-permute-start(bf16[80,384]{1,0:T(8,128)(2,1)S(1)} %direction.1.refs_8_), channel_id=1, source_target_pairs={{0,12},{4,8},{8,4},{12,0},{16,28},{20,24},{24,20},{28,16},{1,13},{... | collective-permute-start | bytes 184328 | tf_op jit(solution)/shard_map/ppermute | solution.py:266
  62.3 4.9 %collective-permute-start.17 = (bf16[80,384]{1,0:T(8,128)(2,1)S(1)}, bf16[80,384]{1,0:T(8,128)(2,1)S(1)}, u32[]{:S(2)}, u32[]{:S(2)}) collective-permute-start(bf16[80,384]{1,0:T(8,128)(2,1)S(1)} %direction.1.refs_8_), channel_id=1, source_target_pairs={{0,8},{4,12},{8,0},{12,4},{16,24},{20,28},{24,16},{28,20},{1,9},{5... | collective-permute-start | bytes 184328 | tf_op jit(solution)/shard_map/ppermute | solution.py:266
  63.3 3.9 %collective-permute-start.16 = (bf16[80,384]{1,0:T(8,128)(2,1)S(1)}, bf16[80,384]{1,0:T(8,128)(2,1)S(1)}, u32[]{:S(2)}, u32[]{:S(2)}) collective-permute-start(bf16[80,384]{1,0:T(8,128)(2,1)S(1)} %direction.1.refs_8_), channel_id=1, source_target_pairs={{0,4},{4,0},{8,12},{12,8},{16,20},{20,16},{24,28},{28,24},{1,5},{5... | collective-permute-start | bytes 184328 | tf_op jit(solution)/shard_map/ppermute | solution.py:266
  67.5 6.3 %collective-permute-start.23 = (bf16[64,384]{1,0:T(8,128)(2,1)S(1)}, bf16[64,384]{1,0:T(8,128)(2,1)S(1)}, u32[]{:S(2)}, u32[]{:S(2)}) collective-permute-start(bf16[64,384]{1,0:T(8,128)(2,1)S(1)} %get-tuple-element.54), channel_id=1, source_target_pairs={{0,1},{1,0},{2,3},{3,2},{4,5},{5,4},{6,7},{7,6},{8,9},{9,8},{10,11... | collective-permute-start | bytes 147464 | tf_op jit(solution)/shard_map/ppermute | solution.py:266
  68.9 5.2 %collective-permute-start.24 = (bf16[64,384]{1,0:T(8,128)(2,1)S(1)}, bf16[64,384]{1,0:T(8,128)(2,1)S(1)}, u32[]{:S(2)}, u32[]{:S(2)}) collective-permute-start(bf16[64,384]{1,0:T(8,128)(2,1)S(1)} %get-tuple-element.55), channel_id=1, source_target_pairs={{0,2},{1,3},{2,0},{3,1},{4,6},{5,7},{6,4},{7,5},{8,10},{9,11},{10,... | collective-permute-start | bytes 147464 | tf_op jit(solution)/shard_map/ppermute | solution.py:266
  71.8 5.9 %collective-permute-start.25 = (bf16[64,384]{1,0:T(8,128)(2,1)S(1)}, bf16[64,384]{1,0:T(8,128)(2,1)S(1)}, u32[]{:S(2)}, u32[]{:S(2)}) collective-permute-start(bf16[64,384]{1,0:T(8,128)(2,1)S(1)} %get-tuple-element.56), channel_id=1, source_target_pairs={{0,3},{1,2},{2,1},{3,0},{4,7},{5,6},{6,5},{7,4},{8,11},{9,10},{10,... | collective-permute-start | bytes 147464 | tf_op jit(solution)/shard_map/ppermute | solution.py:266

commit v2 on v1

v2 whole, which is shorter than its diff:
```python
import functools
import math

import jax
import jax.numpy as jnp
from jax import lax
from jax.experimental import pallas as pl
from jax.experimental.pallas import tpu as pltpu
from jax.sharding import PartitionSpec as P


STUDENT_TEMP = 0.1
TEACHER_TEMP = 0.07
LOSS_SCALE = 524288.0
EPSILON = 1e-06
LOG2E = math.log2(math.e)
LN2 = math.log(2.0)
SCALE_S = LOG2E / STUDENT_TEMP
SCALE_T = LOG2E / TEACHER_TEMP
LANES = 128
NT = (((1,), (1,)), ((), ()))
TN = (((0,), (0,)), ((), ()))
F32 = jnp.float32
BF16 = jnp.bfloat16
VMEM = pl.BlockSpec(memory_space=pltpu.VMEM)
HBM = pl.BlockSpec(memory_space=pltpu.HBM)


def dot(a, b, dims=(((1,), (0,)), ((), ()))):
    return lax.dot_general(a, b, dims, preferred_element_type=F32)


def params(mib):
    return pltpu.CompilerParams(vmem_limit_bytes=mib * 2**20)


def cost(flops, nbytes):
    return pl.CostEstimate(flops=int(flops), bytes_accessed=int(nbytes), transcendentals=0)


def shapes(*specs):
    return tuple(jax.ShapeDtypeStruct(s, d) for s, d in specs)


def route(devices):
    held, stages, bit = [(k, 0) for k in range(devices)], [], 1
    while bit < devices:
        send = [x for x in held if x[0] & bit]
        keep = [x for x in held if not x[0] & bit]
        stages.append((bit, held, send, keep))
        held = keep + [(k ^ bit, c ^ bit) for k, c in send]
        bit *= 2
    return stages, [c for _, c in held]


def repack(stage, old_keep, arrived, new_send, new_keep):
    _, held, send, keep = stage
    size = old_keep.shape[0] * 2 // len(held)
    for names, target in ((send, new_send), (keep, new_keep)):
        for index, name in enumerate(names):
            place = held.index(name)
            source = old_keep if place < len(held) // 2 else arrived
            place = place % (len(held) // 2)
            target[index * size : (index + 1) * size, :] = source[place * size : (place + 1) * size, :]


def pick_kernel(stage, early, hidden_hbm, feats_hbm, masks_hbm, weight_hbm, center_hbm, protos_hbm, *refs):
    rows_out, unit_out, radius_out, send_out, keep_out, offset_out, protos_out = refs[:7]
    hidden, feats, masks, weight, picked_out, sems = refs[7:]
    images, patches, _ = hidden.shape
    fetches = [
        pltpu.make_async_copy(source, target, sems.at[index])
        for index, (source, target) in enumerate(
            [(masks_hbm, masks), (feats_hbm, feats)]
            + [(hidden_hbm.at[image], hidden.at[image]) for image in range(images)]
            + [(weight_hbm, weight), (center_hbm, offset_out)]
        )
    ]
    for fetch in fetches:
        fetch.start()
    fetches[0].wait()
    fetches[1].wait()
    count = masks.shape[1]
    rows = images * count
    patch = lax.broadcasted_iota(jnp.int32, (patches, count), 0)
    for image in range(images):
        here = slice(image * count, (image + 1) * count)
        choice = (patch == masks[image : image + 1, :]).astype(F32).T.astype(BF16)
        fetches[2 + image].wait()
        picked_out[here, :] = dot(choice, hidden[image]).astype(BF16)
        feat = dot(choice, feats[image])
        length = jnp.sqrt(jnp.sum(feat * feat, axis=1, keepdims=True) + EPSILON)
        rows_out[rows + image * count : rows + (image + 1) * count, :] = (feat / length).astype(BF16)
    fetches[2 + images].wait()
    head = pltpu.make_async_copy(
        protos_hbm.at[pl.ds(0, early)], protos_out.at[pl.ds(0, early)], sems.at[4 + images]
    )
    head.start()
    raw = dot(picked_out[...], weight[...])
    radius = jnp.sqrt(jnp.sum(raw * raw, axis=1, keepdims=True) + EPSILON)
    unit = raw / radius
    unit_out[...] = unit
    radius_out[...] = jnp.broadcast_to(radius, radius_out.shape)
    rows_out[0:rows, :] = unit.astype(BF16)
    me = lax.axis_index("dp")
    _, _, send, keep = stage
    width = send_out.shape[1]
    for names, target in ((send, send_out), (keep, keep_out)):
        for index, (k, _) in enumerate(names):
            first = pl.multiple_of(jnp.bitwise_xor(me, k) * width, LANES)
            target[index * rows : (index + 1) * rows, :] = picked_out[:, pl.ds(first, width)]
    fetches[3 + images].wait()
    offset_out[...] = offset_out[...] * SCALE_T
    head.wait()


def stats_kernel(parts, block, unroll, early, stage, *refs):
    row_refs, refs = refs[:parts], refs[parts:]
    fetch = early is not None
    if fetch:
        protos, offsets, source, logits, stats, protos_out, sems, *scratch = refs
        protos = protos_out
    elif stage:
        protos, offsets, done, keep, arrived, logits, stats, new_send, new_keep, *scratch = refs
        repack(stage, keep, arrived, new_send, new_keep)
    else:
        protos, offsets, done, logits, stats, *scratch = refs
    both, tops, sums, cross = scratch
    count = protos.shape[0] // block
    ready = early // block if fetch else count

    def copy(number):
        first = number * block
        if not isinstance(first, int):
            first = pl.multiple_of(first, block)
        piece = pl.ds(first, block)
        return pltpu.make_async_copy(source.at[piece], protos.at[piece], sems.at[number])

    if fetch:
        for number in range(ready, count):
            copy(number).start()
    each = row_refs[0].shape[0] // 2
    rows = parts * each
    for index, ref in enumerate(row_refs):
        both[index * each : (index + 1) * each, :] = ref[0:each, :]
        both[rows + index * each : rows + (index + 1) * each, :] = ref[each:, :]
    tops[...] = jnp.full(tops.shape, -jnp.inf, F32)
    sums[...] = jnp.zeros(sums.shape, F32)
    cross[...] = jnp.zeros(cross.shape, F32)
    groups = block // LANES
    chunk = 8

    pieces = max(1, block // 256)
    piece = block // pieces

    def project(base, number, u, part):
        if fetch and part == 0:
            current = number + u
            if isinstance(current, int):
                if current >= ready:
                    copy(current).wait()
            else:
                pl.when(current >= ready)(lambda: copy(current).wait())
        columns = pl.ds(base + u * block + part * piece, piece)
        logits[:, columns] = dot(both[...], protos[columns, :], NT)

    def reduce(base, u, part):
        lanes = [pl.ds(base + u * block + g * LANES, LANES) for g in range(groups)]
        offset = [offsets[:, lane] for lane in lanes]
        for start in range(part * rows // pieces, (part + 1) * rows // pieces, chunk):
            srow = slice(start, start + chunk)
            trow = slice(rows + start, rows + start + chunk)
            s = [logits[srow, lane] * SCALE_S for lane in lanes]
            t = [logits[trow, lane] * SCALE_T - offset[g] for g, lane in enumerate(lanes)]
            old_s, old_t = tops[srow, :], tops[trow, :]
            new_s = functools.reduce(jnp.maximum, s, old_s)
            new_t = functools.reduce(jnp.maximum, t, old_t)
            tops[srow, :] = new_s
            tops[trow, :] = new_t
            fade = jnp.exp2(old_t - new_t)
            e_t = [jnp.exp2(x - new_t) for x in t]
            sums[srow, :] = sums[srow, :] * jnp.exp2(old_s - new_s) + sum(jnp.exp2(x - new_s) for x in s)
            sums[trow, :] = sums[trow, :] * fade + sum(e_t)
            cross[srow, :] = cross[srow, :] * fade + sum(e * x for e, x in zip(e_t, s))

    def step(index, carry):
        base = index * (unroll * block)
        if not isinstance(base, int):
            base = pl.multiple_of(base, unroll * block)
        for u in range(unroll + 1):
            for part in range(pieces):
                if u < unroll:
                    project(base, index * unroll, u, part)
                if u > 0:
                    reduce(base, u - 1, part)
        return carry

    if count == unroll:
        step(0, 0)
    else:
        lax.fori_loop(0, count // unroll, step, 0)
    peak = jnp.max(tops[...], axis=1, keepdims=True)
    shrink = jnp.exp2(tops[...] - peak)
    total = jnp.sum(sums[...] * shrink, axis=1, keepdims=True)
    mixed = jnp.sum(cross[...] * shrink[rows:, :], axis=1, keepdims=True)
    lane = lax.broadcasted_iota(jnp.int32, (rows, LANES), 1)
    table = jnp.where(lane == 0, peak[0:rows], 0.0)
    table = jnp.where(lane == 1, total[0:rows], table)
    table = jnp.where(lane == 2, peak[rows:], table)
    table = jnp.where(lane == 3, total[rows:], table)
    table = jnp.where(lane == 4, mixed, table)
    if not fetch:
        stats[:, 0:rows] = done[...]
        stats[:, rows:] = table.T[0:8, :]
    else:
        stats[...] = table.T[0:8, :]


def back_kernel(devices, factor, block, parts, which, unroll, stage, *refs):
    stat_refs, (logits, protos, offsets), refs = refs[:devices], refs[devices : devices + 3], refs[devices + 3 :]
    if stage:
        keep, arrived, *refs = refs
    outs, (loss, *refs) = refs[:parts], refs[parts:]
    if stage:
        new_send, new_keep, *refs = refs
        repack(stage, keep, arrived, new_send, new_keep)
    total, *grads = refs
    rows = logits.shape[0] // 2
    each = rows // parts
    slots = range(which * parts, (which + 1) * parts)
    stats = [
        jnp.concatenate([ref[:, (j ^ k) * each : ((j ^ k) + 1) * each] for j in slots], axis=1)
        for k, ref in enumerate(stat_refs)
    ]
    peak_s = functools.reduce(jnp.maximum, [x[0:1] for x in stats])
    peak_t = functools.reduce(jnp.maximum, [x[2:3] for x in stats])
    sum_s = sum(x[1:2] * jnp.exp2(x[0:1] - peak_s) for x in stats)
    sum_t = sum(x[3:4] * jnp.exp2(x[2:3] - peak_t) for x in stats)
    cross = sum(x[4:5] * jnp.exp2(x[2:3] - peak_t) for x in stats)
    row_loss = LN2 * peak_s + jnp.log(sum_s) - LN2 * (cross / sum_t)
    loss[...] = jnp.broadcast_to(jnp.sum(row_loss, axis=1, keepdims=True), loss.shape)

    def columns(row):
        return jnp.broadcast_to(row, (LANES, rows)).T

    top_s = columns(peak_s + jnp.log2(sum_s * (1.0 / factor)))
    top_t = columns(peak_t + jnp.log2(sum_t * (1.0 / factor)))
    total[...] = jnp.zeros(total.shape, F32)
    groups = block // LANES
    chunk = 16

    def scale(base, u):
        lanes = [pl.ds(base + u * block + g * LANES, LANES) for g in range(groups)]
        for g, lane in enumerate(lanes):
            offset = offsets[:, lane]
            for start in range(0, rows, chunk):
                srow = slice(start, start + chunk)
                trow = slice(rows + start, rows + start + chunk)
                value = jnp.exp2(logits[srow, lane] * SCALE_S - top_s[srow])
                value = value - jnp.exp2(logits[trow, lane] * SCALE_T - offset - top_t[srow])
                grads[u][srow, g * LANES : (g + 1) * LANES] = value.astype(BF16)

    def step(index, carry):
        base = index * (unroll * block)
        if not isinstance(base, int):
            base = pl.multiple_of(base, unroll * block)
        for u in range(unroll + 1):
            if u < unroll:
                scale(base, u)
            if u > 0:
                first = base + (u - 1) * block
                total[...] += dot(grads[u - 1][...], protos[pl.ds(first, block), :])
        return carry

    if protos.shape[0] == block * unroll:
        step(0, 0)
    else:
        lax.fori_loop(0, protos.shape[0] // (block * unroll), step, 0)
    for part in range(parts):
        outs[part][...] = total[part * each : (part + 1) * each, :].astype(outs[part].dtype)


def direction_kernel(devices, halves, stage, *refs):
    backs, (unit, radius), losses, refs = (
        refs[:devices],
        refs[devices : devices + 2],
        refs[devices + 2 : devices + 2 + halves],
        refs[devices + 2 + halves :],
    )
    if stage:
        keep, arrived, out, new_send, new_keep = refs
        repack(stage, keep, arrived, new_send, new_keep)
    else:
        (out,) = refs
    rows = unit.shape[0]
    back = sum(ref[...].astype(F32) for ref in backs)
    inner = jnp.sum(unit[...] * back, axis=1, keepdims=True)
    out[0:rows, :] = ((back - unit[...] * inner) / radius[:, 0:1]).astype(BF16)
    value = jnp.broadcast_to(sum(ref[0:1, 0:1] for ref in losses), (out.shape[0] - rows, out.shape[1]))
    high = value.astype(BF16).astype(F32)
    middle = (value - high).astype(BF16).astype(F32)
    low = value - high - middle
    row = lax.broadcasted_iota(jnp.int32, value.shape, 0)
    out[rows:, :] = jnp.where(row == 0, high, jnp.where(row == 1, middle, low)).astype(BF16)


def hidden_kernel(direction, weight, out):
    rows = out.shape[0]
    out[...] = dot(direction[0:rows, :], weight[...], NT).astype(BF16)


def head_kernel(dp, proto, total_rows, origins, *refs):
    cols, dirs, refs = refs[:2], refs[2 : 2 + dp], refs[2 + dp :]
    outs, (loss, left, right, result) = refs[:proto], refs[proto:]
    rows = cols[0].shape[0] * 2 // dp
    for index, origin in enumerate(origins):
        source = cols[index // (dp // 2)]
        place = index % (dp // 2)
        left[origin * rows : (origin + 1) * rows, :] = source[place * rows : (place + 1) * rows, :]
    value = jnp.zeros((1, LANES), F32)
    for k in range(dp):
        right[k * rows : (k + 1) * rows, :] = dirs[k][0:rows, :]
        for term in range(3):
            value = value + dirs[k][rows + term : rows + term + 1, 0:LANES].astype(F32)
    loss[...] = jnp.broadcast_to(value * (1.0 / total_rows), loss.shape)
    result[...] = dot(left[...], right[...], TN)
    me = lax.axis_index("proto")
    size = outs[0].shape[0]
    for k in range(proto):
        first = pl.multiple_of(jnp.bitwise_xor(me, k) * size, 8)
        outs[k][...] = result[pl.ds(first, size), :].astype(outs[k].dtype)


def exchange(x, axis, k):
    size = lax.axis_size(axis)
    return lax.ppermute(x, axis, [(i, i ^ k) for i in range(size)])


def per_device(hidden_states, teacher_feats, masks, head_weight, prototypes, center):
    dp, proto = lax.axis_size("dp"), lax.axis_size("proto")
    assert dp in (8, 16) and proto & (proto - 1) == 0
    hid, bot = head_weight.shape
    rows = masks.shape[0] * masks.shape[1]
    local = prototypes.shape[0]
    total_rows = rows * dp * proto
    factor = LOSS_SCALE / (total_rows * STUDENT_TEMP)
    width = hid // dp
    half = proto // 2
    count = half * rows
    block = math.gcd(local, max(LANES, 2**17 // count))
    steps = local // block
    unroll = math.gcd(steps, max(1, 12 * 128 // count))

    stages, origins = route(dp)
    moving = jax.ShapeDtypeStruct((dp // 2 * rows, width), BF16)
    early = block * min(4, steps - 1)
    pick = pl.pallas_call(
        functools.partial(pick_kernel, stages[0], early),
        out_shape=(
            *shapes(((2 * rows, bot), BF16), ((rows, bot), F32), ((rows, LANES), F32)),
            moving,
            moving,
            pltpu.VMEM((1, local), F32),
            pltpu.VMEM((local, bot), BF16),
        ),
        in_specs=[HBM] * 6,
        out_specs=(VMEM,) * 7,
        scratch_shapes=[
            pltpu.VMEM(hidden_states.shape, BF16),
            pltpu.VMEM(teacher_feats.shape, BF16),
            pltpu.VMEM(masks.shape, jnp.int32),
            pltpu.VMEM(head_weight.shape, BF16),
            pltpu.VMEM((rows, hid), BF16),
            pltpu.SemaphoreType.DMA((5 + masks.shape[0],)),
        ],
        compiler_params=params(16),
        cost_estimate=cost(2 * rows * hid * bot, hidden_states.size * 2),
        name="pick",
    )
    table = pltpu.with_memory_space_constraint(prototypes, pltpu.HBM)
    sources = (hidden_states, teacher_feats, masks, head_weight, center.reshape(1, local))
    own, unit, radius, send, keep, offsets, protos = pick(
        *[pltpu.with_memory_space_constraint(x, pltpu.HBM) for x in sources], table
    )
    near = [own] + [exchange(own, "proto", k) for k in range(1, proto)]

    def move(number, send, keep):
        stage = stages[number] if number < len(stages) else None
        if number > len(stages):
            return stage, ()
        return stage, (keep, exchange(send, "dp", stages[number - 1][0]))

    def stats_call(parts, early, stage, protos, *more):
        fetch = early is not None
        return pl.pallas_call(
            functools.partial(stats_kernel, half, block, unroll, early, stage),
            out_shape=(
                pltpu.VMEM((2 * count, local), F32),
                jax.ShapeDtypeStruct((8, count if fetch else 2 * count), F32),
            ) + ((pltpu.VMEM((local, bot), BF16),) if fetch else ()) + ((moving,) * 2 if stage else ()),
            in_specs=[VMEM] * (half + 2) + [HBM if fetch else VMEM] + [VMEM] * (len(more) - 1),
            out_specs=(VMEM,) * (2 + fetch + (2 if stage else 0)),
            input_output_aliases={half: 2} if fetch else {},
            scratch_shapes=([pltpu.SemaphoreType.DMA((steps,))] if fetch else []) + [
                pltpu.VMEM((2 * count, bot), BF16),
                pltpu.VMEM((2 * count, LANES), F32),
                pltpu.VMEM((2 * count, LANES), F32),
                pltpu.VMEM((count, LANES), F32),
            ],
            compiler_params=params(6),
            cost_estimate=cost(4 * count * local * bot * 2, local * bot * 2),
            name="stats",
        )(*parts, protos, offsets, *more)

    first, sums, protos = stats_call(near[:half], early, None, protos, table)
    stage, held = move(1, send, keep)
    second, mine, *moved = stats_call(near[half:], None, stage, protos, sums, *(held if stage else ()))
    if stage:
        send, keep = moved
    others = [mine] + [exchange(mine, "proto", k) for k in range(1, proto)]

    def back_call(which, stage, held):
        return pl.pallas_call(
            functools.partial(back_kernel, proto, factor, block, half, which, unroll, stage),
            out_shape=shapes(*[((rows, bot), F32)] * half, ((8, LANES), F32)) + ((moving,) * 2 if stage else ()),
            in_specs=[VMEM] * (proto + 3 + len(held)),
            out_specs=(VMEM,) * (half + 1 + (2 if stage else 0)),
            scratch_shapes=[pltpu.VMEM((count, bot), F32)] + [pltpu.VMEM((count, block), BF16)] * unroll,
            compiler_params=params(6),
            cost_estimate=cost(2 * count * local * bot * 2, local * bot * 2),
            name="back",
        )(*others, (first, second)[which], protos, offsets, *held)

    far = back_call(1, None, ())
    stage, held = move(2, send, keep)
    close = back_call(0, stage, held if stage else ())
    if stage:
        send, keep = close[half + 1 :]
    parts = list(close[:half]) + list(far[:half])
    backs = [parts[0]] + [exchange(parts[k], "proto", k) for k in range(1, proto)]

    stage, last = move(3, send, keep)
    direction = pl.pallas_call(
        functools.partial(direction_kernel, proto, 2, stage),
        out_shape=shapes(((rows + 8, bot), BF16)) + ((moving,) * 2 if stage else ()),
        in_specs=[VMEM] * (proto + 4 + (2 if stage else 0)),
        out_specs=(VMEM,) * (3 if stage else 1),
        compiler_params=params(4),
        cost_estimate=cost(rows * bot * 16, rows * bot * 16),
        name="direction",
    )(*backs, unit, radius, close[half], far[half], *(last if stage else ()))
    if stage:
        _, last = move(4, *direction[1:])
    direction = direction[0]
    dirs = {0: direction}
    dirs.update({k: exchange(direction, "dp", k) for k in range(2, dp, 2)})
    dirs.update({k + 1: exchange(dirs[k], "dp", 1) for k in range(0, dp, 2)})
    grad_hidden = pl.pallas_call(
        hidden_kernel,
        out_shape=jax.ShapeDtypeStruct((rows, hid), BF16),
        in_specs=[VMEM] * 2,
        out_specs=VMEM,
        compiler_params=params(8),
        cost_estimate=cost(2 * rows * hid * bot, hid * bot * 2),
        name="hidden",
    )(direction, head_weight)

    size = width // proto
    head = pl.pallas_call(
        functools.partial(head_kernel, dp, proto, total_rows, origins),
        out_shape=shapes(
            *[((size, bot), F32 if k == 0 else BF16) for k in range(proto)], ((8, LANES), F32)
        ),
        in_specs=[VMEM] * (2 + dp),
        out_specs=(VMEM,) * (proto + 1),
        scratch_shapes=[
            pltpu.VMEM((dp * rows, width), BF16),
            pltpu.VMEM((dp * rows, bot), BF16),
            pltpu.VMEM((width, bot), F32),
        ],
        compiler_params=params(8),
        cost_estimate=cost(2 * dp * rows * width * bot, dp * rows * bot * 2),
        name="head",
    )(*last, *[dirs[k] for k in range(dp)])
    grad_head = head[0]
    for k in range(1, proto):
        grad_head = grad_head + exchange(head[k], "proto", k).astype(F32)
    return (head[proto][0, 0], grad_hidden, grad_head)


def solution(mesh):
    return jax.shard_map(
        per_device,
        mesh=mesh,
        in_specs=(
            P(("dp", "proto"), None, None),
            P(("dp", "proto"), None, None),
            P(("dp", "proto"), None),
            P(),
            P("proto", None),
            P("proto"),
        ),
        out_specs=(P(), P(("dp", "proto"), None), P(("dp", "proto"), None)),
        check_vma=False,
    )
```

time: 78.5 us -> 66.3 us (0.84)
  starting transfers between devices: 31.3 us -> 24.8 us
  Pallas kernels: 29.5 us -> 25.1 us
  local copies, waits for them, and re-layouts: 1.31 us -> 0.51 us
    ppermute x26 -> x22, starting transfers between devices: 31.3 us -> 24.8 us  [exchange(): return lax.ppermute(x, axis, [(i, i ^ k) for i in range(size)])]
    pallas_call x5, Pallas kernels: 20.8 us -> 17 us  [the longest x2 12.3 us: stats_call(): pl.pallas_call(functools.partial(stats_kernel, half, block, unroll, early...]
    unnamed x4 -> x2, local copies, waits for them, and re-layouts: 0.8 us -> 0.01 us
    ppermute x26 -> x22, waiting for transfers between devices: 14.8 us -> 14.3 us  [exchange(): return lax.ppermute(x, axis, [(i, i ^ k) for i in range(size)])]
  transfers between devices with their start and end apart: 26 -> 22, of which waited for: 12 -> 12; matrix products, arithmetic and copies ran while one was open for 1% -> 1% of each run, Pallas kernels for 20% -> 23%
where the time goes in v2:
time: 66.3 us; the launch traced here: 66.1 us
  Pallas kernels  25.1 us (38%)
  starting transfers between devices  24.8 us (37%)
  waiting for transfers between devices  14.3 us (22%)
  between operations  0.71 us (1%)
  other arithmetic  0.67 us (1%)
    ppermute x22, starting transfers between devices, exchange(): return lax.ppermute(x, axis, [(i, i ^ k) for i in range(size)])  24.8 us
    ppermute x22, waiting for transfers between devices, exchange(): return lax.ppermute(x, axis, [(i, i ^ k) for i in range(size)])  14.3 us
    pallas_call x2, Pallas kernels, stats_call(): pl.pallas_call(functools.partial(stats_kernel, half, block, unroll, early...  12.3 us
    pallas_call x2, Pallas kernels, back_call(): pl.pallas_call(functools.partial(back_kernel, proto, factor, block, half,...  6.82 us
    pallas_call x1, Pallas kernels, per_device(): pick(*[pltpu.with_memory_space_constraint(x, pltpu.HBM) for x in sources]...  4.21 us
  transfers between devices with their start and end apart: 22, of which 12 were waited for; matrix products, arithmetic and copies ran while one was open for 1% of the time, Pallas kernels for 23%

profile of v2, /device:TPU:0, one launch (start us, length us, event | category | flops | bytes accessed | tf_op | source)
XLA Modules:
  0.0 66.1 jit_solution(871338347557347405)
XLA Ops:
  0.6 4.2 %pick.1 = (bf16[128,384]{1,0:T(8,128)(2,1)S(1)}, f32[64,384]{1,0:T(8,128)S(1)}, f32[64,128]{1,0:T(8,128)S(1)}, bf16[256,256]{1,0:T(8,128)(2,1)S(1)}, bf16[256,25...) custom-call(bf16[2,256,2048]{2,1,0:T(8,128)(2,1)} %hidden_hbm.1, ...), custom_call_target="tpu_custom_call" | custom-call | flops 100663296 | bytes 2097152 | tf_op jit(solution)/shard_map/pick/pallas_call | solution.py:382
  4.9 3.1 %collective-permute-start.2 = (bf16[128,384]{1,0:T(8,128)(2,1)S(1)}, bf16[128,384]{1,0:T(8,128)(2,1)S(1)}, u32[]{:S(2)}, u32[]{:S(2)}) collective-permute-start(bf16[128,384]{1,0:T(8,128)(2,1)S(1)} %get-tuple-element.30.refs_0_), channel_id=1, source_target_pairs={{0,1},{1,0},{2,3},{3,2},{4,5},{5,4},{6,7},{7,6},{8,9},{9,8},{10,11... | collective-permute-start | bytes 294920 | tf_op jit(solution)/shard_map/ppermute | solution.py:336
  8.0 2.5 %collective-permute-start.1 = (bf16[128,384]{1,0:T(8,128)(2,1)S(1)}, bf16[128,384]{1,0:T(8,128)(2,1)S(1)}, u32[]{:S(2)}, u32[]{:S(2)}) collective-permute-start(bf16[128,384]{1,0:T(8,128)(2,1)S(1)} %get-tuple-element.30.refs_0_), channel_id=1, source_target_pairs={{0,3},{1,2},{2,1},{3,0},{4,7},{5,6},{6,5},{7,4},{8,11},{9,10},{10,... | collective-permute-start | bytes 294920 | tf_op jit(solution)/shard_map/ppermute | solution.py:336
  10.4 0.1 collective-permute-start
  10.6 0.0 collective-permute-start.3
  10.6 0.2 collective-permute-done.2.refs_1_
  10.8 6.8 %stats.2 = (f32[256,12288]{1,0:T(8,128)S(1)}, f32[8,128]{1,0:T(8,128)S(1)}, bf16[12288,384]{1,0:T(8,128)(2,1)S(1)}) custom-call(bf16[128,384]{1,0:T(8,128)(2,1)S(1)} %get-tuple-element.30.refs_0_, bf16[128,384]{1,0:T(8,128)(2,1)S(1)} %collective-permute-done.2.refs_1_, ...), custom_call_target="tpu_custom_call", output_to_operand_aliasing={{2}: (2, {})} | custom-call | flops 4831838208 | bytes 9437184 | tf_op jit(solution)/shard_map/stats/pallas_call | solution.py:395
  17.6 0.0 collective-permute-done.1.refs_1_
  17.6 1.8 %collective-permute-done.refs_0_ = bf16[128,384]{1,0:T(8,128)(2,1)S(1)} collective-permute-done((bf16[128,384]{1,0:T(8,128)(2,1)S(1)}, bf16[128,384]{1,0:T(8,128)(2,1)S(1)}, u32[]{:S(2)}, u32[]{:S(2)}) %collective-permute-start) | collective-permute-done | bytes 98336 | tf_op jit(solution)/shard_map/ppermute | solution.py:336
  19.4 5.4 %stats.3 = (f32[256,12288]{1,0:T(8,128)S(1)}, f32[8,256]{1,0:T(8,128)S(1)}, bf16[256,256]{1,0:T(8,128)(2,1)S(1)}, bf16[256,256]{1,0:T(8,128)(2,1)S(1)}) custom-call(bf16[128,384]{1,0:T(8,128)(2,1)S(1)} %collective-permute-done.refs_0_, bf16[128,384]{1,0:T(8,128)(2,1)S(1)} %collective-permute-done.1.refs_1_, ...), custom_call_target="tpu_custom_call" | custom-call | flops 4831838208 | bytes 9437184 | tf_op jit(solution)/shard_map/stats/pallas_call | solution.py:395
  24.8 3.2 %collective-permute-start.6 = (f32[8,256]{1,0:T(8,128)S(1)}, f32[8,256]{1,0:T(8,128)S(1)}, u32[]{:S(2)}, u32[]{:S(2)}) collective-permute-start(f32[8,256]{1,0:T(8,128)S(1)} %get-tuple-element.37.refs_0_), channel_id=1, source_target_pairs={{0,3},{1,2},{2,1},{3,0},{4,7},{5,6},{6,5},{7,4},{8,11},{9,10},{10,... | collective-permute-start | bytes 24584 | tf_op jit(solution)/shard_map/ppermute | solution.py:336
  28.0 0.0 collective-permute-start.5
  28.0 1.2 %collective-permute-start.4 = (f32[8,256]{1,0:T(8,128)S(1)}, f32[8,256]{1,0:T(8,128)S(1)}, u32[]{:S(2)}, u32[]{:S(2)}) collective-permute-start(f32[8,256]{1,0:T(8,128)S(1)} %get-tuple-element.37.refs_0_), channel_id=1, source_target_pairs={{0,1},{1,0},{2,3},{3,2},{4,5},{5,4},{6,7},{7,6},{8,9},{9,8},{10,11... | collective-permute-start | bytes 24584 | tf_op jit(solution)/shard_map/ppermute | solution.py:336
  29.2 1.5 %collective-permute-start.7 = (bf16[256,256]{1,0:T(8,128)(2,1)S(1)}, bf16[256,256]{1,0:T(8,128)(2,1)S(1)}, u32[]{:S(2)}, u32[]{:S(2)}) collective-permute-start(bf16[256,256]{1,0:T(8,128)(2,1)S(1)} %get-tuple-element.40), channel_id=1, source_target_pairs={{0,8},{4,12},{8,0},{12,4},{16,24},{20,28},{24,16},{28,20},{1,9},{5... | collective-permute-start | bytes 393224 | tf_op jit(solution)/shard_map/ppermute | solution.py:336
  30.7 0.0 collective-permute-done.6.refs_3_
  30.7 1.8 %collective-permute-done.5.refs_2_ = f32[8,256]{1,0:T(8,128)S(1)} collective-permute-done((f32[8,256]{1,0:T(8,128)S(1)}, f32[8,256]{1,0:T(8,128)S(1)}, u32[]{:S(2)}, u32[]{:S(2)}) %collective-permute-start.5) | collective-permute-done | bytes 8224 | tf_op jit(solution)/shard_map/ppermute | solution.py:336
  32.6 3.5 %back.3 = (f32[64,384]{1,0:T(8,128)S(1)}, f32[64,384]{1,0:T(8,128)S(1)}, f32[8,128]{1,0:T(8,128)S(1)}) custom-call(f32[8,256]{1,0:T(8,128)S(1)} %get-tuple-element.37.refs_0_, f32[8,256]{1,0:T(8,128)S(1)} %collective-permute-done.4.refs_1_, f32[8,256]{1,0:T(8,128)S(1)} %collective-permute-done.5.refs_2_, f32[8,256]{1,0:T(8,128)S(1)} %collective-permute-done.6.refs_3_, ...), custom_call_target="tpu_custom_call" | custom-call | flops 2415919104 | bytes 9437184 | tf_op jit(solution)/shard_map/back/pallas_call | solution.py:423
  36.1 2.1 %collective-permute-start.10 = (f32[64,384]{1,0:T(8,128)S(1)}, f32[64,384]{1,0:T(8,128)S(1)}, u32[]{:S(2)}, u32[]{:S(2)}) collective-permute-start(f32[64,384]{1,0:T(8,128)S(1)} %get-tuple-element.46), channel_id=1, source_target_pairs={{0,2},{1,3},{2,0},{3,1},{4,6},{5,7},{6,4},{7,5},{8,10},{9,11},{10,... | collective-permute-start | bytes 294920 | tf_op jit(solution)/shard_map/ppermute | solution.py:336
  38.2 0.7 collective-permute-start.11
  38.8 0.0 collective-permute-done.7.refs_8_
  38.8 3.3 %back.2 = (f32[64,384]{1,0:T(8,128)S(1)}, f32[64,384]{1,0:T(8,128)S(1)}, f32[8,128]{1,0:T(8,128)S(1)}, bf16[256,256]{1,0:T(8,128)(2,1)S(1)}, bf16[256,256]{1,0:T(8,128)(2,1)S(1)}) custom-call(f32[8,256]{1,0:T(8,128)S(1)} %get-tuple-element.37.refs_0_, f32[8,256]{1,0:T(8,128)S(1)} %collective-permute-done.4.refs_1_, ...), custom_call_target="tpu_custom_call" | custom-call | flops 2415919104 | bytes 9437184 | tf_op jit(solution)/shard_map/back/pallas_call | solution.py:423
  42.1 0.9 %collective-permute-start.9 = (f32[64,384]{1,0:T(8,128)S(1)}, f32[64,384]{1,0:T(8,128)S(1)}, u32[]{:S(2)}, u32[]{:S(2)}) collective-permute-start(f32[64,384]{1,0:T(8,128)S(1)} %get-tuple-element.44), channel_id=1, source_target_pairs={{0,1},{1,0},{2,3},{3,2},{4,5},{5,4},{6,7},{7,6},{8,9},{9,8},{10,11... | collective-permute-start | bytes 294920 | tf_op jit(solution)/shard_map/ppermute | solution.py:336
  43.0 1.5 %collective-permute-start.8 = (bf16[256,256]{1,0:T(8,128)(2,1)S(1)}, bf16[256,256]{1,0:T(8,128)(2,1)S(1)}, u32[]{:S(2)}, u32[]{:S(2)}) collective-permute-start(bf16[256,256]{1,0:T(8,128)(2,1)S(1)} %get-tuple-element.42), channel_id=1, source_target_pairs={{0,16},{4,20},{8,24},{12,28},{16,0},{20,4},{24,8},{28,12},{1,17},{... | collective-permute-start | bytes 393224 | tf_op jit(solution)/shard_map/ppermute | solution.py:336
  44.5 0.0 collective-permute-done.10.refs_2_
  44.5 0.3 collective-permute-done.11.refs_3_
  44.9 1.9 %collective-permute-done.9.refs_1_ = f32[64,384]{1,0:T(8,128)S(1)} collective-permute-done((f32[64,384]{1,0:T(8,128)S(1)}, f32[64,384]{1,0:T(8,128)S(1)}, u32[]{:S(2)}, u32[]{:S(2)}) %collective-permute-start.9) | collective-permute-done | bytes 98336 | tf_op jit(solution)/shard_map/ppermute | solution.py:336
  46.8 0.1 direction.1.refs_2_
  47.0 2.5 %collective-permute-start.17 = (bf16[72,384]{1,0:T(8,128)(2,1)S(1)}, bf16[72,384]{1,0:T(8,128)(2,1)S(1)}, u32[]{:S(2)}, u32[]{:S(2)}) collective-permute-start(bf16[72,384]{1,0:T(8,128)(2,1)S(1)} %direction.1.refs_2_), channel_id=1, source_target_pairs={{0,24},{4,28},{8,16},{12,20},{16,8},{20,12},{24,0},{28,4},{1,25},{... | collective-permute-start | bytes 165896 | tf_op jit(solution)/shard_map/ppermute | solution.py:336
  49.5 0.5 collective-permute-start.15
  50.0 0.5 collective-permute-start.13
  50.5 0.0 collective-permute-start.12
  50.5 1.7 %collective-permute-done.17.refs_8_ = bf16[72,384]{1,0:T(8,128)(2,1)S(1)} collective-permute-done((bf16[72,384]{1,0:T(8,128)(2,1)S(1)}, bf16[72,384]{1,0:T(8,128)(2,1)S(1)}, u32[]{:S(2)}, u32[]{:S(2)}) %collective-permute-start.17) | collective-permute-done | bytes 55328 | tf_op jit(solution)/shard_map/ppermute | solution.py:336
  52.2 0.0 collective-permute-start.18
  52.2 1.4 %collective-permute-done.15.refs_6_ = bf16[72,384]{1,0:T(8,128)(2,1)S(1)} collective-permute-done((bf16[72,384]{1,0:T(8,128)(2,1)S(1)}, bf16[72,384]{1,0:T(8,128)(2,1)S(1)}, u32[]{:S(2)}, u32[]{:S(2)}) %collective-permute-start.15) | collective-permute-done | bytes 55328 | tf_op jit(solution)/shard_map/ppermute | solution.py:336
  53.6 0.5 collective-permute-done.13.refs_4_
  54.1 0.0 collective-permute-start.14
  54.2 0.0 collective-permute-done.8.refs_1_
  54.2 0.7 %collective-permute-done.16.refs_7_ = bf16[72,384]{1,0:T(8,128)(2,1)S(1)} collective-permute-done((bf16[72,384]{1,0:T(8,128)(2,1)S(1)}, bf16[72,384]{1,0:T(8,128)(2,1)S(1)}, u32[]{:S(2)}, u32[]{:S(2)}) %collective-permute-start.16) | collective-permute-done | bytes 55328 | tf_op jit(solution)/shard_map/ppermute | solution.py:336
  54.9 0.5 collective-permute-done.14.refs_5_
  55.4 0.4 head.1
  55.8 0.9 %collective-permute-start.19 = (bf16[64,384]{1,0:T(8,128)(2,1)S(1)}, bf16[64,384]{1,0:T(8,128)(2,1)S(1)}, u32[]{:S(2)}, u32[]{:S(2)}) collective-permute-start(bf16[64,384]{1,0:T(8,128)(2,1)S(1)} %get-tuple-element.54), channel_id=1, source_target_pairs={{0,1},{1,0},{2,3},{3,2},{4,5},{5,4},{6,7},{7,6},{8,9},{9,8},{10,11... | collective-permute-start | bytes 147464 | tf_op jit(solution)/shard_map/ppermute | solution.py:336
  56.6 2.9 %collective-permute-start.20 = (bf16[64,384]{1,0:T(8,128)(2,1)S(1)}, bf16[64,384]{1,0:T(8,128)(2,1)S(1)}, u32[]{:S(2)}, u32[]{:S(2)}) collective-permute-start(bf16[64,384]{1,0:T(8,128)(2,1)S(1)} %get-tuple-element.55), channel_id=1, source_target_pairs={{0,2},{1,3},{2,0},{3,1},{4,6},{5,7},{6,4},{7,5},{8,10},{9,11},{10,... | collective-permute-start | bytes 147464 | tf_op jit(solution)/shard_map/ppermute | solution.py:336
  59.6 0.7 %collective-permute-start.21 = (bf16[64,384]{1,0:T(8,128)(2,1)S(1)}, bf16[64,384]{1,0:T(8,128)(2,1)S(1)}, u32[]{:S(2)}, u32[]{:S(2)}) collective-permute-start(bf16[64,384]{1,0:T(8,128)(2,1)S(1)} %get-tuple-element.56), channel_id=1, source_target_pairs={{0,3},{1,2},{2,1},{3,0},{4,7},{5,6},{6,5},{7,4},{8,11},{9,10},{10,... | collective-permute-start | bytes 147464 | tf_op jit(solution)/shard_map/ppermute | solution.py:336
  60.2 1.3 %hidden.1 = bf16[64,2048]{1,0:T(8,128)(2,1)} custom-call(bf16[72,384]{1,0:T(8,128)(2,1)S(1)} %direction.1.refs_2_, bf16[2048,384]{1,0:T(8,128)(2,1)S(1)} %copy-done), custom_call_target="tpu_custom_call" | custom-call | flops 100663296 | bytes 1572864 | tf_op jit(solution)/shard_map/hidden/pallas_call | solution.py:458
  61.5 0.5 slice.3
  62.1 0.7 %collective-permute-done.20 = bf16[64,384]{1,0:T(8,128)(2,1)S(1)} collective-permute-done((bf16[64,384]{1,0:T(8,128)(2,1)S(1)}, bf16[64,384]{1,0:T(8,128)(2,1)S(1)}, u32[]{:S(2)}, u32[]{:S(2)}) %collective-permute-start.20) | collective-permute-done | bytes 49184 | tf_op jit(solution)/shard_map/ppermute | solution.py:336
  62.7 2.7 %collective-permute-done.21 = bf16[64,384]{1,0:T(8,128)(2,1)S(1)} collective-permute-done((bf16[64,384]{1,0:T(8,128)(2,1)S(1)}, bf16[64,384]{1,0:T(8,128)(2,1)S(1)}, u32[]{:S(2)}, u32[]{:S(2)}) %collective-permute-start.21) | collective-permute-done | bytes 49184 | tf_op jit(solution)/shard_map/ppermute | solution.py:336
  65.4 0.7 %convert_add_fusion = f32[64,384]{1,0:T(8,128)} fusion(bf16[64,384]{1,0:T(8,128)(2,1)S(1)} %collective-permute-done.21, bf16[64,384]{1,0:T(8,128)(2,1)S(1)} %collective-permute-done.20, f32[64,384]{1,0:T(8,128)S(1)} %get-tuple-element.53, bf16[64,384]{1,0:T(8,128)(2,1)S(1)} %collective-permute-done.19), kind=kLoop, calls=%fused_computation | loop fusion | flops 147456 | bytes 344064 | tf_op jit(solution)/shard_map/add | solution.py:487
  (8 shorter events, 0.0 us)
Async XLA Ops:
  4.9 5.9 %collective-permute-start.2 = (bf16[128,384]{1,0:T(8,128)(2,1)S(1)}, bf16[128,384]{1,0:T(8,128)(2,1)S(1)}, u32[]{:S(2)}, u32[]{:S(2)}) collective-permute-start(bf16[128,384]{1,0:T(8,128)(2,1)S(1)} %get-tuple-element.30.refs_0_), channel_id=1, source_target_pairs={{0,1},{1,0},{2,3},{3,2},{4,5},{5,4},{6,7},{7,6},{8,9},{9,8},{10,11... | collective-permute-start | bytes 294920 | tf_op jit(solution)/shard_map/ppermute | solution.py:336
  8.0 9.7 %collective-permute-start.1 = (bf16[128,384]{1,0:T(8,128)(2,1)S(1)}, bf16[128,384]{1,0:T(8,128)(2,1)S(1)}, u32[]{:S(2)}, u32[]{:S(2)}) collective-permute-start(bf16[128,384]{1,0:T(8,128)(2,1)S(1)} %get-tuple-element.30.refs_0_), channel_id=1, source_target_pairs={{0,3},{1,2},{2,1},{3,0},{4,7},{5,6},{6,5},{7,4},{8,11},{9,10},{10,... | collective-permute-start | bytes 294920 | tf_op jit(solution)/shard_map/ppermute | solution.py:336
  10.4 8.9 %collective-permute-start = (bf16[128,384]{1,0:T(8,128)(2,1)S(1)}, bf16[128,384]{1,0:T(8,128)(2,1)S(1)}, u32[]{:S(2)}, u32[]{:S(2)}) collective-permute-start(bf16[128,384]{1,0:T(8,128)(2,1)S(1)} %get-tuple-element.30.refs_0_), channel_id=1, source_target_pairs={{0,2},{1,3},{2,0},{3,1},{4,6},{5,7},{6,4},{7,5},{8,10},{9,11},{10,... | collective-permute-start | bytes 294920 | tf_op jit(solution)/shard_map/ppermute | solution.py:336
  10.6 8.8 %collective-permute-start.3 = (bf16[256,256]{1,0:T(8,128)(2,1)S(1)}, bf16[256,256]{1,0:T(8,128)(2,1)S(1)}, u32[]{:S(2)}, u32[]{:S(2)}) collective-permute-start(bf16[256,256]{1,0:T(8,128)(2,1)S(1)} %get-tuple-element.36), channel_id=1, source_target_pairs={{0,4},{4,0},{8,12},{12,8},{16,20},{20,16},{24,28},{28,24},{1,5},{5... | collective-permute-start | bytes 393224 | tf_op jit(solution)/shard_map/ppermute | solution.py:336
  24.8 5.9 %collective-permute-start.6 = (f32[8,256]{1,0:T(8,128)S(1)}, f32[8,256]{1,0:T(8,128)S(1)}, u32[]{:S(2)}, u32[]{:S(2)}) collective-permute-start(f32[8,256]{1,0:T(8,128)S(1)} %get-tuple-element.37.refs_0_), channel_id=1, source_target_pairs={{0,3},{1,2},{2,1},{3,0},{4,7},{5,6},{6,5},{7,4},{8,11},{9,10},{10,... | collective-permute-start | bytes 24584 | tf_op jit(solution)/shard_map/ppermute | solution.py:336
  28.0 4.5 %collective-permute-start.5 = (f32[8,256]{1,0:T(8,128)S(1)}, f32[8,256]{1,0:T(8,128)S(1)}, u32[]{:S(2)}, u32[]{:S(2)}) collective-permute-start(f32[8,256]{1,0:T(8,128)S(1)} %get-tuple-element.37.refs_0_), channel_id=1, source_target_pairs={{0,2},{1,3},{2,0},{3,1},{4,6},{5,7},{6,4},{7,5},{8,10},{9,11},{10,... | collective-permute-start | bytes 24584 | tf_op jit(solution)/shard_map/ppermute | solution.py:336
  28.0 4.5 %collective-permute-start.4 = (f32[8,256]{1,0:T(8,128)S(1)}, f32[8,256]{1,0:T(8,128)S(1)}, u32[]{:S(2)}, u32[]{:S(2)}) collective-permute-start(f32[8,256]{1,0:T(8,128)S(1)} %get-tuple-element.37.refs_0_), channel_id=1, source_target_pairs={{0,1},{1,0},{2,3},{3,2},{4,5},{5,4},{6,7},{7,6},{8,9},{9,8},{10,11... | collective-permute-start | bytes 24584 | tf_op jit(solution)/shard_map/ppermute | solution.py:336
  29.2 9.6 %collective-permute-start.7 = (bf16[256,256]{1,0:T(8,128)(2,1)S(1)}, bf16[256,256]{1,0:T(8,128)(2,1)S(1)}, u32[]{:S(2)}, u32[]{:S(2)}) collective-permute-start(bf16[256,256]{1,0:T(8,128)(2,1)S(1)} %get-tuple-element.40), channel_id=1, source_target_pairs={{0,8},{4,12},{8,0},{12,4},{16,24},{20,28},{24,16},{28,20},{1,9},{5... | collective-permute-start | bytes 393224 | tf_op jit(solution)/shard_map/ppermute | solution.py:336
  36.1 8.5 %collective-permute-start.10 = (f32[64,384]{1,0:T(8,128)S(1)}, f32[64,384]{1,0:T(8,128)S(1)}, u32[]{:S(2)}, u32[]{:S(2)}) collective-permute-start(f32[64,384]{1,0:T(8,128)S(1)} %get-tuple-element.46), channel_id=1, source_target_pairs={{0,2},{1,3},{2,0},{3,1},{4,6},{5,7},{6,4},{7,5},{8,10},{9,11},{10,... | collective-permute-start | bytes 294920 | tf_op jit(solution)/shard_map/ppermute | solution.py:336
  38.2 6.7 %collective-permute-start.11 = (f32[64,384]{1,0:T(8,128)S(1)}, f32[64,384]{1,0:T(8,128)S(1)}, u32[]{:S(2)}, u32[]{:S(2)}) collective-permute-start(f32[64,384]{1,0:T(8,128)S(1)} %get-tuple-element.47), channel_id=1, source_target_pairs={{0,3},{1,2},{2,1},{3,0},{4,7},{5,6},{6,5},{7,4},{8,11},{9,10},{10,... | collective-permute-start | bytes 294920 | tf_op jit(solution)/shard_map/ppermute | solution.py:336
  38.8 21.4 %copy-start = (bf16[2048,384]{1,0:T(8,128)(2,1)S(1)}, bf16[2048,384]{1,0:T(8,128)(2,1)}, u32[]{:S(2)}) copy-start(bf16[2048,384]{1,0:T(8,128)(2,1)} %weight.1) | copy-start | bytes 4718596
  42.1 4.7 %collective-permute-start.9 = (f32[64,384]{1,0:T(8,128)S(1)}, f32[64,384]{1,0:T(8,128)S(1)}, u32[]{:S(2)}, u32[]{:S(2)}) collective-permute-start(f32[64,384]{1,0:T(8,128)S(1)} %get-tuple-element.44), channel_id=1, source_target_pairs={{0,1},{1,0},{2,3},{3,2},{4,5},{5,4},{6,7},{7,6},{8,9},{9,8},{10,11... | collective-permute-start | bytes 294920 | tf_op jit(solution)/shard_map/ppermute | solution.py:336
  43.0 11.1 %collective-permute-start.8 = (bf16[256,256]{1,0:T(8,128)(2,1)S(1)}, bf16[256,256]{1,0:T(8,128)(2,1)S(1)}, u32[]{:S(2)}, u32[]{:S(2)}) collective-permute-start(bf16[256,256]{1,0:T(8,128)(2,1)S(1)} %get-tuple-element.42), channel_id=1, source_target_pairs={{0,16},{4,20},{8,24},{12,28},{16,0},{20,4},{24,8},{28,12},{1,17},{... | collective-permute-start | bytes 393224 | tf_op jit(solution)/shard_map/ppermute | solution.py:336
  47.0 5.2 %collective-permute-start.17 = (bf16[72,384]{1,0:T(8,128)(2,1)S(1)}, bf16[72,384]{1,0:T(8,128)(2,1)S(1)}, u32[]{:S(2)}, u32[]{:S(2)}) collective-permute-start(bf16[72,384]{1,0:T(8,128)(2,1)S(1)} %direction.1.refs_2_), channel_id=1, source_target_pairs={{0,24},{4,28},{8,16},{12,20},{16,8},{20,12},{24,0},{28,4},{1,25},{... | collective-permute-start | bytes 165896 | tf_op jit(solution)/shard_map/ppermute | solution.py:336
  49.5 4.2 %collective-permute-start.15 = (bf16[72,384]{1,0:T(8,128)(2,1)S(1)}, bf16[72,384]{1,0:T(8,128)(2,1)S(1)}, u32[]{:S(2)}, u32[]{:S(2)}) collective-permute-start(bf16[72,384]{1,0:T(8,128)(2,1)S(1)} %direction.1.refs_2_), channel_id=1, source_target_pairs={{0,16},{4,20},{8,24},{12,28},{16,0},{20,4},{24,8},{28,12},{1,17},{... | collective-permute-start | bytes 165896 | tf_op jit(solution)/shard_map/ppermute | solution.py:336
  50.0 4.2 %collective-permute-start.13 = (bf16[72,384]{1,0:T(8,128)(2,1)S(1)}, bf16[72,384]{1,0:T(8,128)(2,1)S(1)}, u32[]{:S(2)}, u32[]{:S(2)}) collective-permute-start(bf16[72,384]{1,0:T(8,128)(2,1)S(1)} %direction.1.refs_2_), channel_id=1, source_target_pairs={{0,8},{4,12},{8,0},{12,4},{16,24},{20,28},{24,16},{28,20},{1,9},{5... | collective-permute-start | bytes 165896 | tf_op jit(solution)/shard_map/ppermute | solution.py:336
  50.5 3.6 %collective-permute-start.12 = (bf16[72,384]{1,0:T(8,128)(2,1)S(1)}, bf16[72,384]{1,0:T(8,128)(2,1)S(1)}, u32[]{:S(2)}, u32[]{:S(2)}) collective-permute-start(bf16[72,384]{1,0:T(8,128)(2,1)S(1)} %direction.1.refs_2_), channel_id=1, source_target_pairs={{0,4},{4,0},{8,12},{12,8},{16,20},{20,16},{24,28},{28,24},{1,5},{5... | collective-permute-start | bytes 165896 | tf_op jit(solution)/shard_map/ppermute | solution.py:336
  52.2 2.0 %collective-permute-start.18 = (bf16[72,384]{1,0:T(8,128)(2,1)S(1)}, bf16[72,384]{1,0:T(8,128)(2,1)S(1)}, u32[]{:S(2)}, u32[]{:S(2)}) collective-permute-start(bf16[72,384]{1,0:T(8,128)(2,1)S(1)} %collective-permute-done.17.refs_8_), channel_id=1, source_target_pairs={{0,4},{4,0},{8,12},{12,8},{16,20},{20,16},{24,28},{28,24},{1,5},{5... | collective-permute-start | bytes 165896 | tf_op jit(solution)/shard_map/ppermute | solution.py:336
  53.6 1.2 %collective-permute-start.16 = (bf16[72,384]{1,0:T(8,128)(2,1)S(1)}, bf16[72,384]{1,0:T(8,128)(2,1)S(1)}, u32[]{:S(2)}, u32[]{:S(2)}) collective-permute-start(bf16[72,384]{1,0:T(8,128)(2,1)S(1)} %collective-permute-done.15.refs_6_), channel_id=1, source_target_pairs={{0,4},{4,0},{8,12},{12,8},{16,20},{20,16},{24,28},{28,24},{1,5},{5... | collective-permute-start | bytes 165896 | tf_op jit(solution)/shard_map/ppermute | solution.py:336
  54.1 1.2 %collective-permute-start.14 = (bf16[72,384]{1,0:T(8,128)(2,1)S(1)}, bf16[72,384]{1,0:T(8,128)(2,1)S(1)}, u32[]{:S(2)}, u32[]{:S(2)}) collective-permute-start(bf16[72,384]{1,0:T(8,128)(2,1)S(1)} %collective-permute-done.13.refs_4_), channel_id=1, source_target_pairs={{0,4},{4,0},{8,12},{12,8},{16,20},{20,16},{24,28},{28,24},{1,5},{5... | collective-permute-start | bytes 165896 | tf_op jit(solution)/shard_map/ppermute | solution.py:336
  55.8 6.3 %collective-permute-start.19 = (bf16[64,384]{1,0:T(8,128)(2,1)S(1)}, bf16[64,384]{1,0:T(8,128)(2,1)S(1)}, u32[]{:S(2)}, u32[]{:S(2)}) collective-permute-start(bf16[64,384]{1,0:T(8,128)(2,1)S(1)} %get-tuple-element.54), channel_id=1, source_target_pairs={{0,1},{1,0},{2,3},{3,2},{4,5},{5,4},{6,7},{7,6},{8,9},{9,8},{10,11... | collective-permute-start | bytes 147464 | tf_op jit(solution)/shard_map/ppermute | solution.py:336
  56.6 6.1 %collective-permute-start.20 = (bf16[64,384]{1,0:T(8,128)(2,1)S(1)}, bf16[64,384]{1,0:T(8,128)(2,1)S(1)}, u32[]{:S(2)}, u32[]{:S(2)}) collective-permute-start(bf16[64,384]{1,0:T(8,128)(2,1)S(1)} %get-tuple-element.55), channel_id=1, source_target_pairs={{0,2},{1,3},{2,0},{3,1},{4,6},{5,7},{6,4},{7,5},{8,10},{9,11},{10,... | collective-permute-start | bytes 147464 | tf_op jit(solution)/shard_map/ppermute | solution.py:336
  59.6 5.9 %collective-permute-start.21 = (bf16[64,384]{1,0:T(8,128)(2,1)S(1)}, bf16[64,384]{1,0:T(8,128)(2,1)S(1)}, u32[]{:S(2)}, u32[]{:S(2)}) collective-permute-start(bf16[64,384]{1,0:T(8,128)(2,1)S(1)} %get-tuple-element.56), channel_id=1, source_target_pairs={{0,3},{1,2},{2,1},{3,0},{4,7},{5,6},{6,5},{7,4},{8,11},{9,10},{10,... | collective-permute-start | bytes 147464 | tf_op jit(solution)/shard_map/ppermute | solution.py:336

commit v3 on v2

--- a/solution.py
+++ b/solution.py
@@ -91,11 +91,11 @@
         feat = dot(choice, feats[image])
         length = jnp.sqrt(jnp.sum(feat * feat, axis=1, keepdims=True) + EPSILON)
         rows_out[rows + image * count : rows + (image + 1) * count, :] = (feat / length).astype(BF16)
-    fetches[2 + images].wait()
     head = pltpu.make_async_copy(
         protos_hbm.at[pl.ds(0, early)], protos_out.at[pl.ds(0, early)], sems.at[4 + images]
     )
     head.start()
+    fetches[2 + images].wait()
     raw = dot(picked_out[...], weight[...])
     radius = jnp.sqrt(jnp.sum(raw * raw, axis=1, keepdims=True) + EPSILON)
     unit = raw / radius
@@ -157,8 +157,9 @@
         if fetch and part == 0:
             current = number + u
             if isinstance(current, int):
-                if current >= ready:
-                    copy(current).wait()
+                if current >= ready and (current - ready) % 4 == 0:
+                    for next_one in range(current, min(current + 4, count)):
+                        copy(next_one).wait()
             else:
                 pl.when(current >= ready)(lambda: copy(current).wait())
         columns = pl.ds(base + u * block + part * piece, piece)

time: 66.3 us -> 65.4 us (0.986)
  Pallas kernels: 25.1 us -> 24 us
    pallas_call x2, Pallas kernels: 12.3 us -> 11.5 us  [stats_call(): pl.pallas_call(functools.partial(stats_kernel, half, block, unroll, early...]
  transfers between devices with their start and end apart: 22 -> 22, of which waited for: 12 -> 13; matrix products, arithmetic and copies ran while one was open for 1% -> 1% of each run, Pallas kernels for 23% -> 22%
where the time goes in v3:
time: 65.4 us; the launch traced here: 65.2 us
  starting transfers between devices  24.8 us (38%)
  Pallas kernels  24 us (37%)
  waiting for transfers between devices  14.5 us (22%)
  between operations  0.71 us (1%)
  other arithmetic  0.67 us (1%)
    ppermute x22, starting transfers between devices, exchange(): return lax.ppermute(x, axis, [(i, i ^ k) for i in range(size)])  24.8 us
    ppermute x22, waiting for transfers between devices, exchange(): return lax.ppermute(x, axis, [(i, i ^ k) for i in range(size)])  14.5 us
    pallas_call x2, Pallas kernels, stats_call(): pl.pallas_call(functools.partial(stats_kernel, half, block, unroll, early...  11.5 us
    pallas_call x2, Pallas kernels, back_call(): pl.pallas_call(functools.partial(back_kernel, proto, factor, block, half,...  6.81 us
    pallas_call x1, Pallas kernels, per_device(): pick(*[pltpu.with_memory_space_constraint(x, pltpu.HBM) for x in sources]...  3.86 us
    pallas_call x1, Pallas kernels, per_device(): pl.pallas_call(hidden_kernel, out_shape=jax.ShapeDtypeStruct((rows, hid),...  1.31 us
  transfers between devices with their start and end apart: 22, of which 13 were waited for; matrix products, arithmetic and copies ran while one was open for 1% of the time, Pallas kernels for 22%

profile of v3, /device:TPU:0, one launch (start us, length us, event | category | flops | bytes accessed | tf_op | source)
XLA Modules:
  0.0 65.2 jit_solution(13121866772551273408)
XLA Ops:
  0.6 3.9 %pick.1 = (bf16[128,384]{1,0:T(8,128)(2,1)S(1)}, f32[64,384]{1,0:T(8,128)S(1)}, f32[64,128]{1,0:T(8,128)S(1)}, bf16[256,256]{1,0:T(8,128)(2,1)S(1)}, bf16[256,25...) custom-call(bf16[2,256,2048]{2,1,0:T(8,128)(2,1)} %hidden_hbm.1, ...), custom_call_target="tpu_custom_call" | custom-call | flops 100663296 | bytes 2097152 | tf_op jit(solution)/shard_map/pick/pallas_call | solution.py:383
  4.5 3.1 %collective-permute-start.2 = (bf16[128,384]{1,0:T(8,128)(2,1)S(1)}, bf16[128,384]{1,0:T(8,128)(2,1)S(1)}, u32[]{:S(2)}, u32[]{:S(2)}) collective-permute-start(bf16[128,384]{1,0:T(8,128)(2,1)S(1)} %get-tuple-element.30.refs_0_), channel_id=1, source_target_pairs={{0,1},{1,0},{2,3},{3,2},{4,5},{5,4},{6,7},{7,6},{8,9},{9,8},{10,11... | collective-permute-start | bytes 294920 | tf_op jit(solution)/shard_map/ppermute | solution.py:337
  7.6 2.5 %collective-permute-start.1 = (bf16[128,384]{1,0:T(8,128)(2,1)S(1)}, bf16[128,384]{1,0:T(8,128)(2,1)S(1)}, u32[]{:S(2)}, u32[]{:S(2)}) collective-permute-start(bf16[128,384]{1,0:T(8,128)(2,1)S(1)} %get-tuple-element.30.refs_0_), channel_id=1, source_target_pairs={{0,3},{1,2},{2,1},{3,0},{4,7},{5,6},{6,5},{7,4},{8,11},{9,10},{10,... | collective-permute-start | bytes 294920 | tf_op jit(solution)/shard_map/ppermute | solution.py:337
  10.1 0.1 collective-permute-start
  10.2 0.2 collective-permute-done.2.refs_1_
  10.4 6.1 %stats.2 = (f32[256,12288]{1,0:T(8,128)S(1)}, f32[8,128]{1,0:T(8,128)S(1)}, bf16[12288,384]{1,0:T(8,128)(2,1)S(1)}) custom-call(bf16[128,384]{1,0:T(8,128)(2,1)S(1)} %get-tuple-element.30.refs_0_, bf16[128,384]{1,0:T(8,128)(2,1)S(1)} %collective-permute-done.2.refs_1_, ...), custom_call_target="tpu_custom_call", output_to_operand_aliasing={{2}: (2, {})} | custom-call | flops 4831838208 | bytes 9437184 | tf_op jit(solution)/shard_map/stats/pallas_call | solution.py:396
  16.6 0.0 collective-permute-done.1.refs_1_
  16.6 2.5 %collective-permute-done.refs_0_ = bf16[128,384]{1,0:T(8,128)(2,1)S(1)} collective-permute-done((bf16[128,384]{1,0:T(8,128)(2,1)S(1)}, bf16[128,384]{1,0:T(8,128)(2,1)S(1)}, u32[]{:S(2)}, u32[]{:S(2)}) %collective-permute-start) | collective-permute-done | bytes 98336 | tf_op jit(solution)/shard_map/ppermute | solution.py:337
  19.0 5.4 %stats.3 = (f32[256,12288]{1,0:T(8,128)S(1)}, f32[8,256]{1,0:T(8,128)S(1)}, bf16[256,256]{1,0:T(8,128)(2,1)S(1)}, bf16[256,256]{1,0:T(8,128)(2,1)S(1)}) custom-call(bf16[128,384]{1,0:T(8,128)(2,1)S(1)} %collective-permute-done.refs_0_, bf16[128,384]{1,0:T(8,128)(2,1)S(1)} %collective-permute-done.1.refs_1_, ...), custom_call_target="tpu_custom_call" | custom-call | flops 4831838208 | bytes 9437184 | tf_op jit(solution)/shard_map/stats/pallas_call | solution.py:396
  24.4 2.7 %collective-permute-start.6 = (f32[8,256]{1,0:T(8,128)S(1)}, f32[8,256]{1,0:T(8,128)S(1)}, u32[]{:S(2)}, u32[]{:S(2)}) collective-permute-start(f32[8,256]{1,0:T(8,128)S(1)} %get-tuple-element.37.refs_0_), channel_id=1, source_target_pairs={{0,3},{1,2},{2,1},{3,0},{4,7},{5,6},{6,5},{7,4},{8,11},{9,10},{10,... | collective-permute-start | bytes 24584 | tf_op jit(solution)/shard_map/ppermute | solution.py:337
  27.1 0.0 collective-permute-start.5
  27.1 1.7 %collective-permute-start.4 = (f32[8,256]{1,0:T(8,128)S(1)}, f32[8,256]{1,0:T(8,128)S(1)}, u32[]{:S(2)}, u32[]{:S(2)}) collective-permute-start(f32[8,256]{1,0:T(8,128)S(1)} %get-tuple-element.37.refs_0_), channel_id=1, source_target_pairs={{0,1},{1,0},{2,3},{3,2},{4,5},{5,4},{6,7},{7,6},{8,9},{9,8},{10,11... | collective-permute-start | bytes 24584 | tf_op jit(solution)/shard_map/ppermute | solution.py:337
  28.9 1.5 %collective-permute-start.7 = (bf16[256,256]{1,0:T(8,128)(2,1)S(1)}, bf16[256,256]{1,0:T(8,128)(2,1)S(1)}, u32[]{:S(2)}, u32[]{:S(2)}) collective-permute-start(bf16[256,256]{1,0:T(8,128)(2,1)S(1)} %get-tuple-element.40), channel_id=1, source_target_pairs={{0,8},{4,12},{8,0},{12,4},{16,24},{20,28},{24,16},{28,20},{1,9},{5... | collective-permute-start | bytes 393224 | tf_op jit(solution)/shard_map/ppermute | solution.py:337
  30.4 0.0 collective-permute-done.6.refs_3_
  30.4 1.3 %collective-permute-done.5.refs_2_ = f32[8,256]{1,0:T(8,128)S(1)} collective-permute-done((f32[8,256]{1,0:T(8,128)S(1)}, f32[8,256]{1,0:T(8,128)S(1)}, u32[]{:S(2)}, u32[]{:S(2)}) %collective-permute-start.5) | collective-permute-done | bytes 8224 | tf_op jit(solution)/shard_map/ppermute | solution.py:337
  31.7 3.5 %back.3 = (f32[64,384]{1,0:T(8,128)S(1)}, f32[64,384]{1,0:T(8,128)S(1)}, f32[8,128]{1,0:T(8,128)S(1)}) custom-call(f32[8,256]{1,0:T(8,128)S(1)} %get-tuple-element.37.refs_0_, f32[8,256]{1,0:T(8,128)S(1)} %collective-permute-done.4.refs_1_, f32[8,256]{1,0:T(8,128)S(1)} %collective-permute-done.5.refs_2_, f32[8,256]{1,0:T(8,128)S(1)} %collective-permute-done.6.refs_3_, ...), custom_call_target="tpu_custom_call" | custom-call | flops 2415919104 | bytes 9437184 | tf_op jit(solution)/shard_map/back/pallas_call | solution.py:424
  35.2 2.1 %collective-permute-start.10 = (f32[64,384]{1,0:T(8,128)S(1)}, f32[64,384]{1,0:T(8,128)S(1)}, u32[]{:S(2)}, u32[]{:S(2)}) collective-permute-start(f32[64,384]{1,0:T(8,128)S(1)} %get-tuple-element.46), channel_id=1, source_target_pairs={{0,2},{1,3},{2,0},{3,1},{4,6},{5,7},{6,4},{7,5},{8,10},{9,11},{10,... | collective-permute-start | bytes 294920 | tf_op jit(solution)/shard_map/ppermute | solution.py:337
  37.3 1.2 %collective-permute-start.11 = (f32[64,384]{1,0:T(8,128)S(1)}, f32[64,384]{1,0:T(8,128)S(1)}, u32[]{:S(2)}, u32[]{:S(2)}) collective-permute-start(f32[64,384]{1,0:T(8,128)S(1)} %get-tuple-element.47), channel_id=1, source_target_pairs={{0,3},{1,2},{2,1},{3,0},{4,7},{5,6},{6,5},{7,4},{8,11},{9,10},{10,... | collective-permute-start | bytes 294920 | tf_op jit(solution)/shard_map/ppermute | solution.py:337
  38.5 0.0 collective-permute-done.7.refs_8_
  38.5 3.3 %back.2 = (f32[64,384]{1,0:T(8,128)S(1)}, f32[64,384]{1,0:T(8,128)S(1)}, f32[8,128]{1,0:T(8,128)S(1)}, bf16[256,256]{1,0:T(8,128)(2,1)S(1)}, bf16[256,256]{1,0:T(8,128)(2,1)S(1)}) custom-call(f32[8,256]{1,0:T(8,128)S(1)} %get-tuple-element.37.refs_0_, f32[8,256]{1,0:T(8,128)S(1)} %collective-permute-done.4.refs_1_, ...), custom_call_target="tpu_custom_call" | custom-call | flops 2415919104 | bytes 9437184 | tf_op jit(solution)/shard_map/back/pallas_call | solution.py:424
  41.8 0.4 collective-permute-start.9
  42.1 1.5 %collective-permute-start.8 = (bf16[256,256]{1,0:T(8,128)(2,1)S(1)}, bf16[256,256]{1,0:T(8,128)(2,1)S(1)}, u32[]{:S(2)}, u32[]{:S(2)}) collective-permute-start(bf16[256,256]{1,0:T(8,128)(2,1)S(1)} %get-tuple-element.42), channel_id=1, source_target_pairs={{0,16},{4,20},{8,24},{12,28},{16,0},{20,4},{24,8},{28,12},{1,17},{... | collective-permute-start | bytes 393224 | tf_op jit(solution)/shard_map/ppermute | solution.py:337
  43.6 0.1 collective-permute-done.10.refs_2_
  43.7 1.1 %collective-permute-done.11.refs_3_ = f32[64,384]{1,0:T(8,128)S(1)} collective-permute-done((f32[64,384]{1,0:T(8,128)S(1)}, f32[64,384]{1,0:T(8,128)S(1)}, u32[]{:S(2)}, u32[]{:S(2)}) %collective-permute-start.11) | collective-permute-done | bytes 98336 | tf_op jit(solution)/shard_map/ppermute | solution.py:337
  44.8 1.6 %collective-permute-done.9.refs_1_ = f32[64,384]{1,0:T(8,128)S(1)} collective-permute-done((f32[64,384]{1,0:T(8,128)S(1)}, f32[64,384]{1,0:T(8,128)S(1)}, u32[]{:S(2)}, u32[]{:S(2)}) %collective-permute-start.9) | collective-permute-done | bytes 98336 | tf_op jit(solution)/shard_map/ppermute | solution.py:337
  46.5 0.1 direction.1.refs_2_
  46.6 2.5 %collective-permute-start.17 = (bf16[72,384]{1,0:T(8,128)(2,1)S(1)}, bf16[72,384]{1,0:T(8,128)(2,1)S(1)}, u32[]{:S(2)}, u32[]{:S(2)}) collective-permute-start(bf16[72,384]{1,0:T(8,128)(2,1)S(1)} %direction.1.refs_2_), channel_id=1, source_target_pairs={{0,24},{4,28},{8,16},{12,20},{16,8},{20,12},{24,0},{28,4},{1,25},{... | collective-permute-start | bytes 165896 | tf_op jit(solution)/shard_map/ppermute | solution.py:337
  49.1 0.5 collective-permute-start.15
  49.6 0.5 collective-permute-start.13
  50.1 0.0 collective-permute-start.12
  50.1 2.0 %collective-permute-done.17.refs_8_ = bf16[72,384]{1,0:T(8,128)(2,1)S(1)} collective-permute-done((bf16[72,384]{1,0:T(8,128)(2,1)S(1)}, bf16[72,384]{1,0:T(8,128)(2,1)S(1)}, u32[]{:S(2)}, u32[]{:S(2)}) %collective-permute-start.17) | collective-permute-done | bytes 55328 | tf_op jit(solution)/shard_map/ppermute | solution.py:337
  52.1 1.1 %collective-permute-done.15.refs_6_ = bf16[72,384]{1,0:T(8,128)(2,1)S(1)} collective-permute-done((bf16[72,384]{1,0:T(8,128)(2,1)S(1)}, bf16[72,384]{1,0:T(8,128)(2,1)S(1)}, u32[]{:S(2)}, u32[]{:S(2)}) %collective-permute-start.15) | collective-permute-done | bytes 55328 | tf_op jit(solution)/shard_map/ppermute | solution.py:337
  53.3 0.0 collective-permute-start.16
  53.3 0.5 collective-permute-done.13.refs_4_
  53.8 0.0 collective-permute-start.14
  53.8 0.0 collective-permute-done.8.refs_1_
  53.8 0.0 collective-permute-done.12.refs_3_
  53.8 0.7 %collective-permute-done.16.refs_7_ = bf16[72,384]{1,0:T(8,128)(2,1)S(1)} collective-permute-done((bf16[72,384]{1,0:T(8,128)(2,1)S(1)}, bf16[72,384]{1,0:T(8,128)(2,1)S(1)}, u32[]{:S(2)}, u32[]{:S(2)}) %collective-permute-start.16) | collective-permute-done | bytes 55328 | tf_op jit(solution)/shard_map/ppermute | solution.py:337
  54.5 0.5 collective-permute-done.14.refs_5_
  55.0 0.4 head.1
  55.4 0.3 collective-permute-start.19
  55.7 2.9 %collective-permute-start.20 = (bf16[64,384]{1,0:T(8,128)(2,1)S(1)}, bf16[64,384]{1,0:T(8,128)(2,1)S(1)}, u32[]{:S(2)}, u32[]{:S(2)}) collective-permute-start(bf16[64,384]{1,0:T(8,128)(2,1)S(1)} %get-tuple-element.55), channel_id=1, source_target_pairs={{0,2},{1,3},{2,0},{3,1},{4,6},{5,7},{6,4},{7,5},{8,10},{9,11},{10,... | collective-permute-start | bytes 147464 | tf_op jit(solution)/shard_map/ppermute | solution.py:337
  58.7 1.2 %collective-permute-start.21 = (bf16[64,384]{1,0:T(8,128)(2,1)S(1)}, bf16[64,384]{1,0:T(8,128)(2,1)S(1)}, u32[]{:S(2)}, u32[]{:S(2)}) collective-permute-start(bf16[64,384]{1,0:T(8,128)(2,1)S(1)} %get-tuple-element.56), channel_id=1, source_target_pairs={{0,3},{1,2},{2,1},{3,0},{4,7},{5,6},{6,5},{7,4},{8,11},{9,10},{10,... | collective-permute-start | bytes 147464 | tf_op jit(solution)/shard_map/ppermute | solution.py:337
  59.8 1.3 %hidden.1 = bf16[64,2048]{1,0:T(8,128)(2,1)} custom-call(bf16[72,384]{1,0:T(8,128)(2,1)S(1)} %direction.1.refs_2_, bf16[2048,384]{1,0:T(8,128)(2,1)S(1)} %copy-done), custom_call_target="tpu_custom_call" | custom-call | flops 100663296 | bytes 1572864 | tf_op jit(solution)/shard_map/hidden/pallas_call | solution.py:459
  61.2 0.5 slice.3
  61.7 0.4 collective-permute-done.20
  62.1 2.4 %collective-permute-done.21 = bf16[64,384]{1,0:T(8,128)(2,1)S(1)} collective-permute-done((bf16[64,384]{1,0:T(8,128)(2,1)S(1)}, bf16[64,384]{1,0:T(8,128)(2,1)S(1)}, u32[]{:S(2)}, u32[]{:S(2)}) %collective-permute-start.21) | collective-permute-done | bytes 49184 | tf_op jit(solution)/shard_map/ppermute | solution.py:337
  64.5 0.7 %convert_add_fusion = f32[64,384]{1,0:T(8,128)} fusion(bf16[64,384]{1,0:T(8,128)(2,1)S(1)} %collective-permute-done.21, bf16[64,384]{1,0:T(8,128)(2,1)S(1)} %collective-permute-done.20, f32[64,384]{1,0:T(8,128)S(1)} %get-tuple-element.53, bf16[64,384]{1,0:T(8,128)(2,1)S(1)} %collective-permute-done.19), kind=kLoop, calls=%fused_computation | loop fusion | flops 147456 | bytes 344064 | tf_op jit(solution)/shard_map/add | solution.py:488
  (8 shorter events, 0.0 us)
Async XLA Ops:
  4.5 5.9 %collective-permute-start.2 = (bf16[128,384]{1,0:T(8,128)(2,1)S(1)}, bf16[128,384]{1,0:T(8,128)(2,1)S(1)}, u32[]{:S(2)}, u32[]{:S(2)}) collective-permute-start(bf16[128,384]{1,0:T(8,128)(2,1)S(1)} %get-tuple-element.30.refs_0_), channel_id=1, source_target_pairs={{0,1},{1,0},{2,3},{3,2},{4,5},{5,4},{6,7},{7,6},{8,9},{9,8},{10,11... | collective-permute-start | bytes 294920 | tf_op jit(solution)/shard_map/ppermute | solution.py:337
  7.6 8.9 %collective-permute-start.1 = (bf16[128,384]{1,0:T(8,128)(2,1)S(1)}, bf16[128,384]{1,0:T(8,128)(2,1)S(1)}, u32[]{:S(2)}, u32[]{:S(2)}) collective-permute-start(bf16[128,384]{1,0:T(8,128)(2,1)S(1)} %get-tuple-element.30.refs_0_), channel_id=1, source_target_pairs={{0,3},{1,2},{2,1},{3,0},{4,7},{5,6},{6,5},{7,4},{8,11},{9,10},{10,... | collective-permute-start | bytes 294920 | tf_op jit(solution)/shard_map/ppermute | solution.py:337
  10.1 8.9 %collective-permute-start = (bf16[128,384]{1,0:T(8,128)(2,1)S(1)}, bf16[128,384]{1,0:T(8,128)(2,1)S(1)}, u32[]{:S(2)}, u32[]{:S(2)}) collective-permute-start(bf16[128,384]{1,0:T(8,128)(2,1)S(1)} %get-tuple-element.30.refs_0_), channel_id=1, source_target_pairs={{0,2},{1,3},{2,0},{3,1},{4,6},{5,7},{6,4},{7,5},{8,10},{9,11},{10,... | collective-permute-start | bytes 294920 | tf_op jit(solution)/shard_map/ppermute | solution.py:337
  10.2 8.8 %collective-permute-start.3 = (bf16[256,256]{1,0:T(8,128)(2,1)S(1)}, bf16[256,256]{1,0:T(8,128)(2,1)S(1)}, u32[]{:S(2)}, u32[]{:S(2)}) collective-permute-start(bf16[256,256]{1,0:T(8,128)(2,1)S(1)} %get-tuple-element.36), channel_id=1, source_target_pairs={{0,4},{4,0},{8,12},{12,8},{16,20},{20,16},{24,28},{28,24},{1,5},{5... | collective-permute-start | bytes 393224 | tf_op jit(solution)/shard_map/ppermute | solution.py:337
  24.4 5.9 %collective-permute-start.6 = (f32[8,256]{1,0:T(8,128)S(1)}, f32[8,256]{1,0:T(8,128)S(1)}, u32[]{:S(2)}, u32[]{:S(2)}) collective-permute-start(f32[8,256]{1,0:T(8,128)S(1)} %get-tuple-element.37.refs_0_), channel_id=1, source_target_pairs={{0,3},{1,2},{2,1},{3,0},{4,7},{5,6},{6,5},{7,4},{8,11},{9,10},{10,... | collective-permute-start | bytes 24584 | tf_op jit(solution)/shard_map/ppermute | solution.py:337
  27.1 4.5 %collective-permute-start.5 = (f32[8,256]{1,0:T(8,128)S(1)}, f32[8,256]{1,0:T(8,128)S(1)}, u32[]{:S(2)}, u32[]{:S(2)}) collective-permute-start(f32[8,256]{1,0:T(8,128)S(1)} %get-tuple-element.37.refs_0_), channel_id=1, source_target_pairs={{0,2},{1,3},{2,0},{3,1},{4,6},{5,7},{6,4},{7,5},{8,10},{9,11},{10,... | collective-permute-start | bytes 24584 | tf_op jit(solution)/shard_map/ppermute | solution.py:337
  27.1 4.5 %collective-permute-start.4 = (f32[8,256]{1,0:T(8,128)S(1)}, f32[8,256]{1,0:T(8,128)S(1)}, u32[]{:S(2)}, u32[]{:S(2)}) collective-permute-start(f32[8,256]{1,0:T(8,128)S(1)} %get-tuple-element.37.refs_0_), channel_id=1, source_target_pairs={{0,1},{1,0},{2,3},{3,2},{4,5},{5,4},{6,7},{7,6},{8,9},{9,8},{10,11... | collective-permute-start | bytes 24584 | tf_op jit(solution)/shard_map/ppermute | solution.py:337
  28.9 9.6 %collective-permute-start.7 = (bf16[256,256]{1,0:T(8,128)(2,1)S(1)}, bf16[256,256]{1,0:T(8,128)(2,1)S(1)}, u32[]{:S(2)}, u32[]{:S(2)}) collective-permute-start(bf16[256,256]{1,0:T(8,128)(2,1)S(1)} %get-tuple-element.40), channel_id=1, source_target_pairs={{0,8},{4,12},{8,0},{12,4},{16,24},{20,28},{24,16},{28,20},{1,9},{5... | collective-permute-start | bytes 393224 | tf_op jit(solution)/shard_map/ppermute | solution.py:337
  35.2 8.5 %collective-permute-start.10 = (f32[64,384]{1,0:T(8,128)S(1)}, f32[64,384]{1,0:T(8,128)S(1)}, u32[]{:S(2)}, u32[]{:S(2)}) collective-permute-start(f32[64,384]{1,0:T(8,128)S(1)} %get-tuple-element.46), channel_id=1, source_target_pairs={{0,2},{1,3},{2,0},{3,1},{4,6},{5,7},{6,4},{7,5},{8,10},{9,11},{10,... | collective-permute-start | bytes 294920 | tf_op jit(solution)/shard_map/ppermute | solution.py:337
  37.3 7.5 %collective-permute-start.11 = (f32[64,384]{1,0:T(8,128)S(1)}, f32[64,384]{1,0:T(8,128)S(1)}, u32[]{:S(2)}, u32[]{:S(2)}) collective-permute-start(f32[64,384]{1,0:T(8,128)S(1)} %get-tuple-element.47), channel_id=1, source_target_pairs={{0,3},{1,2},{2,1},{3,0},{4,7},{5,6},{6,5},{7,4},{8,11},{9,10},{10,... | collective-permute-start | bytes 294920 | tf_op jit(solution)/shard_map/ppermute | solution.py:337
  38.5 21.4 %copy-start = (bf16[2048,384]{1,0:T(8,128)(2,1)S(1)}, bf16[2048,384]{1,0:T(8,128)(2,1)}, u32[]{:S(2)}) copy-start(bf16[2048,384]{1,0:T(8,128)(2,1)} %weight.1) | copy-start | bytes 4718596
  41.8 4.7 %collective-permute-start.9 = (f32[64,384]{1,0:T(8,128)S(1)}, f32[64,384]{1,0:T(8,128)S(1)}, u32[]{:S(2)}, u32[]{:S(2)}) collective-permute-start(f32[64,384]{1,0:T(8,128)S(1)} %get-tuple-element.44), channel_id=1, source_target_pairs={{0,1},{1,0},{2,3},{3,2},{4,5},{5,4},{6,7},{7,6},{8,9},{9,8},{10,11... | collective-permute-start | bytes 294920 | tf_op jit(solution)/shard_map/ppermute | solution.py:337
  42.1 11.7 %collective-permute-start.8 = (bf16[256,256]{1,0:T(8,128)(2,1)S(1)}, bf16[256,256]{1,0:T(8,128)(2,1)S(1)}, u32[]{:S(2)}, u32[]{:S(2)}) collective-permute-start(bf16[256,256]{1,0:T(8,128)(2,1)S(1)} %get-tuple-element.42), channel_id=1, source_target_pairs={{0,16},{4,20},{8,24},{12,28},{16,0},{20,4},{24,8},{28,12},{1,17},{... | collective-permute-start | bytes 393224 | tf_op jit(solution)/shard_map/ppermute | solution.py:337
  46.6 5.5 %collective-permute-start.17 = (bf16[72,384]{1,0:T(8,128)(2,1)S(1)}, bf16[72,384]{1,0:T(8,128)(2,1)S(1)}, u32[]{:S(2)}, u32[]{:S(2)}) collective-permute-start(bf16[72,384]{1,0:T(8,128)(2,1)S(1)} %direction.1.refs_2_), channel_id=1, source_target_pairs={{0,24},{4,28},{8,16},{12,20},{16,8},{20,12},{24,0},{28,4},{1,25},{... | collective-permute-start | bytes 165896 | tf_op jit(solution)/shard_map/ppermute | solution.py:337
  49.1 4.2 %collective-permute-start.15 = (bf16[72,384]{1,0:T(8,128)(2,1)S(1)}, bf16[72,384]{1,0:T(8,128)(2,1)S(1)}, u32[]{:S(2)}, u32[]{:S(2)}) collective-permute-start(bf16[72,384]{1,0:T(8,128)(2,1)S(1)} %direction.1.refs_2_), channel_id=1, source_target_pairs={{0,16},{4,20},{8,24},{12,28},{16,0},{20,4},{24,8},{28,12},{1,17},{... | collective-permute-start | bytes 165896 | tf_op jit(solution)/shard_map/ppermute | solution.py:337
  49.6 4.2 %collective-permute-start.13 = (bf16[72,384]{1,0:T(8,128)(2,1)S(1)}, bf16[72,384]{1,0:T(8,128)(2,1)S(1)}, u32[]{:S(2)}, u32[]{:S(2)}) collective-permute-start(bf16[72,384]{1,0:T(8,128)(2,1)S(1)} %direction.1.refs_2_), channel_id=1, source_target_pairs={{0,8},{4,12},{8,0},{12,4},{16,24},{20,28},{24,16},{28,20},{1,9},{5... | collective-permute-start | bytes 165896 | tf_op jit(solution)/shard_map/ppermute | solution.py:337
  50.1 3.7 %collective-permute-start.12 = (bf16[72,384]{1,0:T(8,128)(2,1)S(1)}, bf16[72,384]{1,0:T(8,128)(2,1)S(1)}, u32[]{:S(2)}, u32[]{:S(2)}) collective-permute-start(bf16[72,384]{1,0:T(8,128)(2,1)S(1)} %direction.1.refs_2_), channel_id=1, source_target_pairs={{0,4},{4,0},{8,12},{12,8},{16,20},{20,16},{24,28},{28,24},{1,5},{5... | collective-permute-start | bytes 165896 | tf_op jit(solution)/shard_map/ppermute | solution.py:337
  52.1 1.7 %collective-permute-start.18 = (bf16[72,384]{1,0:T(8,128)(2,1)S(1)}, bf16[72,384]{1,0:T(8,128)(2,1)S(1)}, u32[]{:S(2)}, u32[]{:S(2)}) collective-permute-start(bf16[72,384]{1,0:T(8,128)(2,1)S(1)} %collective-permute-done.17.refs_8_), channel_id=1, source_target_pairs={{0,4},{4,0},{8,12},{12,8},{16,20},{20,16},{24,28},{28,24},{1,5},{5... | collective-permute-start | bytes 165896 | tf_op jit(solution)/shard_map/ppermute | solution.py:337
  53.3 1.2 %collective-permute-start.16 = (bf16[72,384]{1,0:T(8,128)(2,1)S(1)}, bf16[72,384]{1,0:T(8,128)(2,1)S(1)}, u32[]{:S(2)}, u32[]{:S(2)}) collective-permute-start(bf16[72,384]{1,0:T(8,128)(2,1)S(1)} %collective-permute-done.15.refs_6_), channel_id=1, source_target_pairs={{0,4},{4,0},{8,12},{12,8},{16,20},{20,16},{24,28},{28,24},{1,5},{5... | collective-permute-start | bytes 165896 | tf_op jit(solution)/shard_map/ppermute | solution.py:337
  53.8 1.2 %collective-permute-start.14 = (bf16[72,384]{1,0:T(8,128)(2,1)S(1)}, bf16[72,384]{1,0:T(8,128)(2,1)S(1)}, u32[]{:S(2)}, u32[]{:S(2)}) collective-permute-start(bf16[72,384]{1,0:T(8,128)(2,1)S(1)} %collective-permute-done.13.refs_4_), channel_id=1, source_target_pairs={{0,4},{4,0},{8,12},{12,8},{16,20},{20,16},{24,28},{28,24},{1,5},{5... | collective-permute-start | bytes 165896 | tf_op jit(solution)/shard_map/ppermute | solution.py:337
  55.4 6.3 %collective-permute-start.19 = (bf16[64,384]{1,0:T(8,128)(2,1)S(1)}, bf16[64,384]{1,0:T(8,128)(2,1)S(1)}, u32[]{:S(2)}, u32[]{:S(2)}) collective-permute-start(bf16[64,384]{1,0:T(8,128)(2,1)S(1)} %get-tuple-element.54), channel_id=1, source_target_pairs={{0,1},{1,0},{2,3},{3,2},{4,5},{5,4},{6,7},{7,6},{8,9},{9,8},{10,11... | collective-permute-start | bytes 147464 | tf_op jit(solution)/shard_map/ppermute | solution.py:337
  55.7 6.4 %collective-permute-start.20 = (bf16[64,384]{1,0:T(8,128)(2,1)S(1)}, bf16[64,384]{1,0:T(8,128)(2,1)S(1)}, u32[]{:S(2)}, u32[]{:S(2)}) collective-permute-start(bf16[64,384]{1,0:T(8,128)(2,1)S(1)} %get-tuple-element.55), channel_id=1, source_target_pairs={{0,2},{1,3},{2,0},{3,1},{4,6},{5,7},{6,4},{7,5},{8,10},{9,11},{10,... | collective-permute-start | bytes 147464 | tf_op jit(solution)/shard_map/ppermute | solution.py:337
  58.7 5.9 %collective-permute-start.21 = (bf16[64,384]{1,0:T(8,128)(2,1)S(1)}, bf16[64,384]{1,0:T(8,128)(2,1)S(1)}, u32[]{:S(2)}, u32[]{:S(2)}) collective-permute-start(bf16[64,384]{1,0:T(8,128)(2,1)S(1)} %get-tuple-element.56), channel_id=1, source_target_pairs={{0,3},{1,2},{2,1},{3,0},{4,7},{5,6},{6,5},{7,4},{8,11},{9,10},{10,... | collective-permute-start | bytes 147464 | tf_op jit(solution)/shard_map/ppermute | solution.py:337
